TPU v7x, 32 devices: a whole 2x2x4 slice. The times are simulated.
32 devices in a mesh: gx: 4 (over y, x), gy: 8 (over z, core).
Axes of the slice: x: 2, y: 2, z: 4, core: 2. Of those that a mesh axis runs over, the one named last changes fastest.
Arguments:
- positions: float32 [3, 65536], P(None, ('gx', 'gy')), may hold values from 0 to 4
- node_moments: float32 [10, 16384], P(None, ('gx', 'gy')), as said below
- slot_of: int32 [32, 2048], P(('gx', 'gy')), may hold values from 0 to 2047, each once within a row
- block_list: int32 [512, 16], P(('gx', 'gy')), may hold values from 0 to 127, as said below
- tile_counts: int32 [512], P(('gx', 'gy')), may hold values from 1 to 16, as said below
Outputs:
- accel: float32 [3, 65536], P(None, ('gx', 'gy'))
Inputs may be any that keep to these rules, and one draw needn't show every extreme that they name: `block_list`: each row names 16 different node blocks; only a tile's first tile_counts entries are used. `tile_counts`: some tile of every draw uses all 16 slots. `node_moments`: masses lie in 0.02 to 0.2 and centres in 0 to 4.
All inputs are finite; a program needn't handle non-finite values.
Results may differ from a plain program's by a relative error of at most 0.0003.
Values sent between devices are 32-bit elements; how exact they have to be, the bound alone decides.
No kernel may reach another device: no remote copies, remote signals or barrier semaphores. Data moves between devices by JAX's collectives and lax.ppermute only.
A program may use at most 64 MiB of HBM per device.

v0:
```python
import functools
import math

import jax
import jax.numpy as jnp
from jax import lax
from jax.experimental import pallas as pl
from jax.experimental.pallas import tpu as pltpu
from jax.sharding import PartitionSpec as P

LANES = 128
SUBS = 8
PAIRS = 8
FEATURES = 48
WEIGHTS = 40
split_a = 0.5
soft_sq = 0.25
root_pi = math.sqrt(math.pi)

ERFC_BIAS = 0.15
ERFC_POLY = (
    0.565651365,
    -0.0323440266,
    1.41906215,
    -1.34343713,
    0.938636763,
    -0.36025162,
    0.0669870813,
)

UNIT = split_a * split_a / math.log(2.0)
LEAD = ERFC_POLY[-1] * UNIT ** ((len(ERFC_POLY) - 1) / 2)
MONIC = tuple(coef * UNIT ** (i / 2) / LEAD for i, coef in enumerate(ERFC_POLY))[:-1]
BIAS = ERFC_BIAS * UNIT
SCALE = LEAD * UNIT
ADD_2 = 4.0 * split_a**3 / root_pi / 3.0 / SCALE
ADD_3 = 8.0 * split_a**5 / root_pi / 15.0 / (SCALE * UNIT)


def thirds(value):
    top = value.astype(jnp.bfloat16).astype(jnp.float32)
    rest = value - top
    mid = rest.astype(jnp.bfloat16).astype(jnp.float32)
    low = (rest - mid).astype(jnp.bfloat16).astype(jnp.float32)
    return top, mid, low


def quotient(value, by):
    if by & (by - 1) == 0:
        return lax.shift_right_logical(value, by.bit_length() - 1)
    return lax.div(value, by)


def hot_lanes(slots, count):
    lane = lax.bitwise_and(slots, LANES - 1)
    rows = lax.broadcasted_iota(jnp.int32, (LANES, count), 0)
    return jnp.where(rows == lane, 1.0, 0.0).astype(jnp.bfloat16)


def owners(slots, tiles, count):
    rows = lax.broadcasted_iota(jnp.int32, (tiles, count), 0)
    return rows == lax.shift_right_logical(slots, 7)


def prep_kernel(pos_ref, slot_ref, tiled_ref, origin_ref, left_ref, rows_ref):
    count = pos_ref.shape[1]
    tiles = count // LANES
    slots = slot_ref[...]
    owner = owners(slots, tiles, count)
    hot = hot_lanes(slots, count)
    place = []
    for c in range(3):
        value = pos_ref[c : c + 1, :]
        origin = jnp.sum(value, axis=1, keepdims=True) * (1.0 / count)
        origin_ref[c : c + 1, :] = jnp.broadcast_to(origin, (1, LANES))
        value = value - origin
        total = None
        for part in thirds(value):
            rows = jnp.where(owner, part, 0.0).astype(jnp.bfloat16)
            got = lax.dot_general(
                rows, hot, (((1,), (1,)), ((), ())), preferred_element_type=jnp.float32
            )
            total = got if total is None else total + got
        tiled_ref[c] = total
        place.append(total)
    x, y, z = place
    one = jnp.ones_like(x)
    zero = jnp.zeros_like(x)
    terms = [x, y, z, one, -UNIT * (x * x + y * y + (z * z + soft_sq)), x, y, z]
    terms += [x * x, y * y, z * z, x * y, x * z, y * z, one, zero]
    for i, term in enumerate(terms):
        top, mid, low = thirds(term)
        for s, part in enumerate((top, top, top, mid, mid, low)):
            rows_ref[pl.ds(s * 16 + i, tiles, stride=LANES), :] = part
    for s in range(96, LANES):
        rows_ref[pl.ds(s, tiles, stride=LANES), :] = zero
    for t in range(tiles):
        left_ref[t] = rows_ref[pl.ds(t * LANES, LANES), :].T.astype(jnp.bfloat16)


def node_features(origin_ref, nodes_ref, feats_ref, weights_ref):
    devices, rows, _ = nodes_ref.shape
    each = rows // 10
    group = max(1, SUBS // each)
    wide = group * each
    shape = (wide, LANES)
    centre = [jnp.broadcast_to(origin_ref[c : c + 1, :], shape) for c in range(3)]

    def some(i, carry):
        def row(r):
            parts = [
                nodes_ref[i * group + g, r * each : (r + 1) * each, :] for g in range(group)
            ]
            return parts[0] if group == 1 else jnp.concatenate(parts, axis=0)

        def put(ref, high, r, value):
            ref[pl.ds(i * (wide * high) + r, wide, stride=high), :] = value

        mass = row(0)
        cx, cy, cz = (row(1 + c) - centre[c] for c in range(3))
        qxx, qyy, qzz, qxy, qxz, qyz = (row(4 + c) for c in range(6))
        vx = qxx * cx + qxy * cy + qxz * cz
        vy = qxy * cx + qyy * cy + qyz * cz
        vz = qxz * cx + qyz * cy + qzz * cz
        terms = [2.0 * UNIT * cx, 2.0 * UNIT * cy, 2.0 * UNIT * cz]
        terms += [-UNIT * (cx * cx + cy * cy + cz * cz)]
        one, two = 7.5 * UNIT**2, 15.0 * UNIT**2
        terms += [jnp.ones(shape, jnp.float32), -two * vx, -two * vy, -two * vz]
        terms += [one * qxx, one * qyy, one * qzz, two * qxy, two * qxz, two * qyz]
        terms += [one * (vx * cx + vy * cy + vz * cz)]
        for r, term in enumerate(terms):
            for s, part in enumerate(thirds(term)):
                put(feats_ref, FEATURES, s * 16 + r, part)
        for s in range(3):
            put(feats_ref, FEATURES, s * 16 + 15, mass)
        half = (1.5 * UNIT) * (qxx + qyy + qzz)
        full = 3.0 * UNIT
        diag = [full * qxx + half, full * qyy + half, full * qzz + half]
        near = [full * vx + half * cx, full * vy + half * cy, full * vz + half * cz]
        zero = jnp.zeros(shape, jnp.float32)
        for c, value in enumerate((cx, cy, cz)):
            for s, part in enumerate(thirds(value)):
                put(weights_ref, WEIGHTS, s * 3 + c, part)
        put(weights_ref, WEIGHTS, 9, zero + 1.0)
        for r in range(10, 16):
            put(weights_ref, WEIGHTS, r, zero)
        for c, value in enumerate(near):
            for s, part in enumerate(thirds(value)):
                put(weights_ref, WEIGHTS, 16 + s * 3 + c, -part)
        put(weights_ref, WEIGHTS, 25, zero)
        for c, value in enumerate(diag + [full * qxy, full * qxz, full * qyz]):
            top, mid, _ = thirds(value)
            put(weights_ref, WEIGHTS, 26 + c, top)
            put(weights_ref, WEIGHTS, 32 + c, mid)
        put(weights_ref, WEIGHTS, 38, zero)
        put(weights_ref, WEIGHTS, 39, zero)
        return carry

    lax.fori_loop(0, devices // group, some, 0)


def distances(left, feats_ref, block, near_ref):
    base = pl.multiple_of(block * FEATURES, SUBS)
    rows = lax.broadcasted_iota(jnp.int32, (SUBS, LANES), 0)
    zero = jnp.zeros((SUBS, LANES), jnp.float32)
    first, second = [], []
    for s in range(3):
        one = feats_ref[pl.ds(base + s * 16, SUBS), :]
        two = feats_ref[pl.ds(base + s * 16 + SUBS, SUBS), :]
        first.append(jnp.concatenate([jnp.where(rows < 5, one, 0.0), zero], axis=0))
        second.append(
            jnp.concatenate(
                [jnp.where(rows >= 5, one, 0.0), jnp.where(rows < 7, two, 0.0)], axis=0
            )
        )
    blank = jnp.zeros((LANES - 96, 2 * LANES), jnp.float32)
    order = (0, 1, 2, 0, 1, 0)
    right = jnp.concatenate(
        [jnp.concatenate([first[s], second[s]], axis=1) for s in order] + [blank], axis=0
    ).astype(jnp.bfloat16)
    near_ref[...] = jnp.dot(left, right, preferred_element_type=jnp.float32)


def pair_terms(near_ref, feats_ref, block, terms_ref):
    mass = feats_ref[pl.ds(block * FEATURES + 15, 1), :]
    step = 2 * SUBS
    for g in range(LANES // step):
        at = pl.ds(g * step, step)
        power = near_ref[at, 0:LANES]
        inner = near_ref[at, LANES : 2 * LANES]
        inv = lax.rsqrt(power * power)
        expo = jnp.exp2(power)
        arg = lax.rsqrt(BIAS - power)
        poly = arg + MONIC[-1]
        for coef in MONIC[-2::-1]:
            poly = poly * arg + coef
        first = poly * inv
        second = (first + ADD_2) * inv
        third = (second + ADD_3) * inv
        radial = (mass * first + third * inner) * expo
        second = second * expo
        for i, value in enumerate((radial, second)):
            top = value.astype(jnp.bfloat16)
            low = (value - top.astype(jnp.float32)).astype(jnp.bfloat16)
            terms_ref[i, at, :] = top
            terms_ref[2 + i, at, :] = low


def add_forces(terms_ref, weights_ref, block, total_ref, tile):
    base = pl.multiple_of(block * WEIGHTS, SUBS)
    top = jnp.concatenate(
        [weights_ref[pl.ds(base, 16), :], jnp.zeros((SUBS, LANES), jnp.float32)], axis=0
    )
    low = weights_ref[pl.ds(base + 16, 24), :]
    right = jnp.concatenate([top, low, top, low], axis=1).astype(jnp.bfloat16)
    left = jnp.concatenate([terms_ref[i] for i in range(4)], axis=1)
    got = lax.dot_general(
        left, right, (((1,), (1,)), ((), ())), preferred_element_type=jnp.float32
    )
    total_ref[tile, :, 0:24] += got


def main_kernel(
    gx,
    gy,
    lists_ref,
    counts_ref,
    tiled_ref,
    origin_ref,
    left_ref,
    slot_ref,
    nodes_ref,
    out_ref,
    feats_ref,
    weights_ref,
    near_ref,
    terms_ref,
    total_ref,
    flat_ref,
):
    count = slot_ref.shape[1]
    tiles = count // LANES
    each = nodes_ref.shape[1] // 10
    node_features(origin_ref, nodes_ref, feats_ref, weights_ref)
    total_ref[...] = jnp.zeros_like(total_ref)
    live = lax.fori_loop(0, tiles, lambda t, n: n + counts_ref[t], 0)

    def take(t, k):
        row = jnp.minimum(t, tiles - 1)
        block = lists_ref[row, k]
        dev = quotient(block, each)
        place = (dev % gy) * gx + quotient(dev, gy)
        block = place * each + block % each
        wrap = k + 1 >= counts_ref[row]
        return row, jnp.minimum(t, tiles), block, jnp.where(wrap, t + 1, t), jnp.where(wrap, 0, k + 1)

    def ahead(u, t, k):
        row, tile, block, t, k = take(t, k)
        distances(left_ref[row], feats_ref, block, near_ref.at[u])
        return (tile, block), t, k

    def behind(u, pair):
        add_forces(terms_ref.at[u], weights_ref, pair[1], total_ref, pair[0])

    def step(i, carry):
        t, k, pairs, last = carry
        nexts = []
        behind(PAIRS - 1, last)
        for u in range(PAIRS):
            pair_terms(near_ref.at[u], feats_ref, pairs[u][1], terms_ref.at[u])
            pair, t, k = ahead(u, t, k)
            nexts.append(pair)
            if u + 1 < PAIRS:
                behind(u, pairs[u])
        return t, k, tuple(nexts), pairs[-1]

    t, k, pairs = jnp.int32(0), jnp.int32(0), []
    for u in range(PAIRS):
        pair, t, k = ahead(u, t, k)
        pairs.append(pair)
    none = (jnp.int32(tiles), jnp.int32(0))
    terms_ref[PAIRS - 1] = jnp.zeros(terms_ref.shape[1:], terms_ref.dtype)
    steps = lax.div(live + (PAIRS - 1), PAIRS)
    carry = lax.fori_loop(0, steps, step, (t, k, tuple(pairs), none))
    behind(PAIRS - 1, carry[-1])

    for t in range(tiles):
        flat_ref[pl.ds(t * LANES, LANES), :] = total_ref[t].T

    def column(r):
        return flat_ref[pl.ds(r, tiles, stride=LANES), :]

    x, y, z = tiled_ref[0], tiled_ref[1], tiled_ref[2]
    sums = column(9)
    mxx, myy, mzz, mxy, mxz, myz = (column(10 + c) + column(16 + c) for c in range(6))
    const = [column(c) + column(3 + c) + column(6 + c) for c in range(3)]
    forces = [
        SCALE * (const[0] - x * sums + (mxx * x + mxy * y + mxz * z)),
        SCALE * (const[1] - y * sums + (mxy * x + myy * y + myz * z)),
        SCALE * (const[2] - z * sums + (mxz * x + myz * y + mzz * z)),
    ]
    slots = slot_ref[...]
    owner = owners(slots, tiles, count)
    hot = hot_lanes(slots, count)
    for c in range(3):
        total = None
        for part in thirds(forces[c]):
            got = jnp.dot(part.astype(jnp.bfloat16), hot, preferred_element_type=jnp.float32)
            total = got if total is None else total + got
        out_ref[c : c + 1, :] = jnp.sum(jnp.where(owner, total, 0.0), axis=0, keepdims=True)


def shards(gx, gy, positions, node_moments, slot_of, block_list, tile_counts):
    count = positions.shape[1]
    tiles = count // LANES
    each = node_moments.shape[1] // LANES
    blocks = each * gx * gy
    packed = node_moments.reshape(10 * each, LANES)
    vmem = pl.BlockSpec(memory_space=pltpu.VMEM)
    smem = pl.BlockSpec(memory_space=pltpu.SMEM)
    tiled, origin, left = pl.pallas_call(
        prep_kernel,
        out_shape=(
            jax.ShapeDtypeStruct((3, tiles, LANES), jnp.float32),
            jax.ShapeDtypeStruct((3, LANES), jnp.float32),
            jax.ShapeDtypeStruct((tiles, LANES, LANES), jnp.bfloat16),
        ),
        in_specs=[vmem] * 2,
        out_specs=(vmem,) * 3,
        scratch_shapes=[pltpu.VMEM((tiles * LANES, LANES), jnp.float32)],
    )(positions, slot_of)
    every = lax.all_gather(packed, "gx", axis=0)
    every = lax.all_gather(every, "gy", axis=0)
    every = every.reshape(gx * gy, 10 * each, LANES)
    return pl.pallas_call(
        functools.partial(main_kernel, gx, gy),
        out_shape=jax.ShapeDtypeStruct((3, count), jnp.float32),
        in_specs=[smem] * 2 + [vmem] * 5,
        out_specs=vmem,
        scratch_shapes=[
            pltpu.VMEM((blocks * FEATURES, LANES), jnp.float32),
            pltpu.VMEM((blocks * WEIGHTS, LANES), jnp.float32),
            pltpu.VMEM((PAIRS, LANES, 2 * LANES), jnp.float32),
            pltpu.VMEM((PAIRS, 4, LANES, LANES), jnp.bfloat16),
            pltpu.VMEM((tiles + 1, LANES, LANES), jnp.float32),
            pltpu.VMEM((tiles * LANES, LANES), jnp.float32),
        ],
    )(block_list, tile_counts, tiled, origin, left, slot_of, every)


def solution(mesh):
    placed = (
        P(None, ("gx", "gy")),
        P(None, ("gx", "gy")),
        P(("gx", "gy"), None),
        P(("gx", "gy"), None),
        P(("gx", "gy")),
    )
    return jax.shard_map(
        functools.partial(shards, mesh.shape["gx"], mesh.shape["gy"]),
        mesh=mesh,
        in_specs=placed,
        out_specs=P(None, ("gx", "gy")),
        check_vma=False,
    )
```

profile of v0, /device:TPU:13, one launch (start us, length us, event | category | flops | bytes accessed | tf_op | source)
XLA Modules:
  0.0 52.2 jit_solution(6444949931648596665)
XLA Ops:
  0.0 0.8 %all_gather_reshape.3 = f32[1,40,128]{2,1,0:T(8,128)S(1)} reshape(f32[10,512]{1,0:T(8,128)} %param.6) | data formatting | bytes 40960 | tf_op jit(solution)/shard_map/all_gather;reshape | solution.py:332
  0.8 6.3 %all_gather.9 = f32[4,40,128]{2,1,0:T(8,128)S(1)} all-gather(f32[1,40,128]{2,1,0:T(8,128)S(1)} %all_gather_reshape.3), channel_id=1, replica_groups=mesh['gx'=4,'gy'=8] {'gx'}, dimensions={0}, use_global_device_ids=true | all-gather | bytes 102400 | tf_op jit(solution)/shard_map/all_gather | solution.py:332
  7.1 3.8 %shard_map.55 = (f32[3,16,128]{2,1,0:T(8,128)}, f32[3,128]{1,0:T(4,128)}, bf16[16,128,128]{2,1,0:T(8,128)(2,1)}) custom-call(f32[3,2048]{1,0:T(4,128)} %pos_ref.1, s32[1,2048]{1,0:T(1,128)} %slot_ref.3), custom_call_target="tpu_custom_call" | custom-call | tf_op jit(solution)/shard_map/pallas_call | solution.py:321
  10.9 18.8 %all-gather.nodes_ref = f32[32,40,128]{2,1,0:T(8,128)} all-gather(f32[4,40,128]{2,1,0:T(8,128)S(1)} %all_gather.9), channel_id=2, replica_groups=mesh['gx'=4,'gy'=8] {'gy'}, dimensions={0}, use_global_device_ids=true | all-gather | bytes 737280 | tf_op jit(solution)/shard_map/all_gather | solution.py:333
  29.7 22.5 %shard_map.56 = f32[3,2048]{1,0:T(4,128)} custom-call(s32[16,16]{1,0:T(8,128)} %lists_ref.1, s32[16]{0:T(128)} %counts_ref.1, f32[3,16,128]{2,1,0:T(8,128)} %get-tuple-element.8.tiled_ref, f32[3,128]{1,0:T(4,128)} %get-tuple-element.9.origin_ref, bf16[16,128,128]{2,1,0:T(8,128)(2,1)} %get-tuple-element.10.left_ref, s32[1,2048]{1,0:T(1,128)} %slot_ref.3, ...), custom_call_target="tpu_custom_call" | custom-call | tf_op jit(solution)/shard_map/pallas_call | solution.py:335
where the time goes:
time: 52.1 us; the launch traced here: 52.2 us
  Pallas kernels  26.3 us (50%)
  blocking collectives  25 us (48%)
  local copies, waits for them, and re-layouts  0.76 us (1%)
    pallas_call x1, Pallas kernels, shards(): pl.pallas_call(functools.partial(main_kernel, gx, gy), out_shape=jax.Shap...  22.5 us
    all_gather x1, blocking collectives, shards(): every = lax.all_gather(every, 'gy', axis=0)  18.8 us
    all_gather x1, blocking collectives, shards(): every = lax.all_gather(packed, 'gx', axis=0)  6.29 us
    pallas_call x1, Pallas kernels, shards(): pl.pallas_call(prep_kernel, out_shape=(jax.ShapeDtypeStruct((3, tiles, LA...  3.84 us

commit v1 on v0

--- a/solution.py
+++ b/solution.py
@@ -98,7 +98,7 @@
         left_ref[t] = rows_ref[pl.ds(t * LANES, LANES), :].T.astype(jnp.bfloat16)
 
 
-def node_features(origin_ref, nodes_ref, feats_ref, weights_ref):
+def node_features(origin_ref, nodes_ref, feats_ref, weights_ref, start):
     devices, rows, _ = nodes_ref.shape
     each = rows // 10
     group = max(1, SUBS // each)
@@ -114,7 +114,7 @@
             return parts[0] if group == 1 else jnp.concatenate(parts, axis=0)
 
         def put(ref, high, r, value):
-            ref[pl.ds(i * (wide * high) + r, wide, stride=high), :] = value
+            ref[pl.ds((start + i * wide) * high + r, wide, stride=high), :] = value
 
         mass = row(0)
         cx, cy, cz = (row(1 + c) - centre[c] for c in range(3))
@@ -225,11 +225,13 @@
     gy,
     lists_ref,
     counts_ref,
+    self_ref,
     tiled_ref,
     origin_ref,
     left_ref,
     slot_ref,
-    nodes_ref,
+    mine_ref,
+    twin_ref,
     out_ref,
     feats_ref,
     weights_ref,
@@ -240,8 +242,11 @@
 ):
     count = slot_ref.shape[1]
     tiles = count // LANES
-    each = nodes_ref.shape[1] // 10
-    node_features(origin_ref, nodes_ref, feats_ref, weights_ref)
+    each = mine_ref.shape[1] // 10
+    half = mine_ref.shape[0] * each
+    node_features(origin_ref, mine_ref, feats_ref, weights_ref, 0)
+    node_features(origin_ref, twin_ref, feats_ref, weights_ref, half)
+    my_x, my_y = self_ref[0], self_ref[1]
     total_ref[...] = jnp.zeros_like(total_ref)
     live = lax.fori_loop(0, tiles, lambda t, n: n + counts_ref[t], 0)
 
@@ -249,8 +254,9 @@
         row = jnp.minimum(t, tiles - 1)
         block = lists_ref[row, k]
         dev = quotient(block, each)
-        place = (dev % gy) * gx + quotient(dev, gy)
-        block = place * each + block % each
+        far_x = quotient(dev, gy) ^ my_x
+        far_y = (dev & (gy - 1)) ^ my_y
+        block = ((far_y >> 1) * gx + far_x) * each + (block & (each - 1)) + (far_y & 1) * half
         wrap = k + 1 >= counts_ref[row]
         return row, jnp.minimum(t, tiles), block, jnp.where(wrap, t + 1, t), jnp.where(wrap, 0, k + 1)
 
@@ -315,9 +321,15 @@
     tiles = count // LANES
     each = node_moments.shape[1] // LANES
     blocks = each * gx * gy
-    packed = node_moments.reshape(10 * each, LANES)
     vmem = pl.BlockSpec(memory_space=pltpu.VMEM)
     smem = pl.BlockSpec(memory_space=pltpu.SMEM)
+    def swap(value, axis, size, bits):
+        return lax.ppermute(value, axis, [(i, i ^ bits) for i in range(size)])
+
+    near = [node_moments] + [swap(node_moments, "gx", gx, b) for b in range(1, gx)]
+    near = jnp.stack([value.reshape(10 * each, LANES) for value in near])
+    near, positions = lax.optimization_barrier((near, positions))
+    far = [swap(near, "gy", gy, b) for b in range(2, gy, 2)]
     tiled, origin, left = pl.pallas_call(
         prep_kernel,
         out_shape=(
@@ -328,14 +340,20 @@
         in_specs=[vmem] * 2,
         out_specs=(vmem,) * 3,
         scratch_shapes=[pltpu.VMEM((tiles * LANES, LANES), jnp.float32)],
+        compiler_params=pltpu.CompilerParams(vmem_limit_bytes=8 * 2**20),
+        cost_estimate=pl.CostEstimate(flops=10**10, bytes_accessed=10**6, transcendentals=0),
     )(positions, slot_of)
-    every = lax.all_gather(packed, "gx", axis=0)
-    every = lax.all_gather(every, "gy", axis=0)
-    every = every.reshape(gx * gy, 10 * each, LANES)
+    mine = jnp.concatenate([near] + far, axis=0)
+    mine, origin = lax.optimization_barrier((mine, origin))
+    twin = swap(mine, "gy", gy, 1)
+    row = 4 * LANES
+    limit = row * (blocks * (FEATURES + WEIGHTS + 10) + PAIRS * 4 * LANES + tiles * 3 * LANES)
+    limit = min(limit + 2**21, 60 * 1024 * 1024)
+    here = jnp.stack([lax.axis_index("gx"), lax.axis_index("gy")]).astype(jnp.int32)
     return pl.pallas_call(
         functools.partial(main_kernel, gx, gy),
         out_shape=jax.ShapeDtypeStruct((3, count), jnp.float32),
-        in_specs=[smem] * 2 + [vmem] * 5,
+        in_specs=[smem] * 3 + [vmem] * 6,
         out_specs=vmem,
         scratch_shapes=[
             pltpu.VMEM((blocks * FEATURES, LANES), jnp.float32),
@@ -345,7 +363,8 @@
             pltpu.VMEM((tiles + 1, LANES, LANES), jnp.float32),
             pltpu.VMEM((tiles * LANES, LANES), jnp.float32),
         ],
-    )(block_list, tile_counts, tiled, origin, left, slot_of, every)
+        compiler_params=pltpu.CompilerParams(vmem_limit_bytes=limit),
+    )(block_list, tile_counts, here, tiled, origin, left, slot_of, mine, twin)
 
 
 def solution(mesh):

time: 52.1 us -> 39 us (0.75)
  the two profiles are of different devices: /device:TPU:13 before, /device:TPU:3 now
where the time goes in v1:
time: 39 us; the launch traced here: 38.8 us
  Pallas kernels  21.5 us (55%)
  waiting for transfers between devices  7.91 us (20%)
  starting transfers between devices  7.71 us (20%)
  local copies, waits for them, and re-layouts  1.47 us (4%)
    pallas_call x1, Pallas kernels, shards(): pl.pallas_call(functools.partial(main_kernel, gx, gy), out_shape=jax.Shap...  19.3 us
    ppermute x7, waiting for transfers between devices, swap(): return lax.ppermute(value, axis, [(i, i ^ bits) for i in range(size)])  7.91 us
    ppermute x7, starting transfers between devices, swap(): return lax.ppermute(value, axis, [(i, i ^ bits) for i in range(size)])  7.71 us
    pallas_call x1, Pallas kernels, shards(): pl.pallas_call(prep_kernel, out_shape=(jax.ShapeDtypeStruct((3, tiles, LA...  2.28 us
    another operation x4, local copies, waits for them, and re-layouts, shards(): near = jnp.stack([value.reshape(10 * each, LANES) for value in near])  0.81 us
  transfers between devices with their start and end apart: 7, of which 4 were waited for; matrix products, arithmetic and copies ran while one was open for 2% of the time, Pallas kernels for 6%

profile of v1, /device:TPU:3, one launch (start us, length us, event | category | flops | bytes accessed | tf_op | source)
XLA Modules:
  0.0 38.8 jit_solution(7733398246170454044)
XLA Ops:
  0.0 0.0 collective-permute-start
  0.0 2.4 %collective-permute-start.2 = (f32[10,512]{1,0:T(8,128)}, f32[10,512]{1,0:T(8,128)S(1)}, u32[]{:S(2)}, u32[]{:S(2)}) collective-permute-start(f32[10,512]{1,0:T(8,128)} %param.6), channel_id=1, source_target_pairs={{0,24},{8,16},{16,8},{24,0},{1,25},{9,17},{17,9},{25,1},{2,26},{10... | collective-permute-start | bytes 61448 | tf_op jit(solution)/shard_map/ppermute | solution.py:327
  2.4 0.2 collective-permute-start.1
  2.7 0.8 %stack_reshape.12 = f32[1,40,128]{2,1,0:T(8,128)S(1)} reshape(f32[10,512]{1,0:T(8,128)} %param.6) | data formatting | bytes 40960 | tf_op jit(solution)/shard_map/stack;reshape | solution.py:330
  3.4 0.0 collective-permute-done
  3.5 0.8 %collective-permute-done.2 = f32[10,512]{1,0:T(8,128)S(1)} collective-permute-done((f32[10,512]{1,0:T(8,128)}, f32[10,512]{1,0:T(8,128)S(1)}, u32[]{:S(2)}, u32[]{:S(2)}) %collective-permute-start.2) | collective-permute-done | bytes 20512 | tf_op jit(solution)/shard_map/ppermute | solution.py:327
  4.3 1.5 %collective-permute-done.1 = f32[10,512]{1,0:T(8,128)S(1)} collective-permute-done((f32[10,512]{1,0:T(8,128)}, f32[10,512]{1,0:T(8,128)S(1)}, u32[]{:S(2)}, u32[]{:S(2)}) %collective-permute-start.1) | collective-permute-done | bytes 20512 | tf_op jit(solution)/shard_map/ppermute | solution.py:327
  5.8 0.0 copy-start.1
  5.8 0.0 copy-start.3
  5.8 3.5 %collective-permute-start.5 = (f32[4,40,128]{2,1,0:T(8,128)S(1)}, f32[4,40,128]{2,1,0:T(8,128)S(1)}, u32[]{:S(2)}, u32[]{:S(2)}) collective-permute-start(f32[4,40,128]{2,1,0:T(8,128)S(1)} %pad_maximum_fusion.1), channel_id=1, source_target_pairs={{0,6},{1,7},{2,4},{3,5},{4,2},{5,3},{6,0},{7,1},{8,14},{9,15},{10,... | collective-permute-start | bytes 245768 | tf_op jit(solution)/shard_map/ppermute | solution.py:327
  9.3 0.0 collective-permute-start.4
  9.3 0.4 collective-permute-start.3
  9.6 0.0 copy-done.1
  9.6 0.0 copy-done.3
  9.6 2.3 %shard_map.55 = (f32[3,16,128]{2,1,0:T(8,128)S(1)}, f32[3,128]{1,0:T(4,128)S(1)}, bf16[16,128,128]{2,1,0:T(8,128)(2,1)S(1)}) custom-call(f32[3,2048]{1,0:T(4,128)S(1)} %copy-done.3, s32[1,2048]{1,0:T(1,128)S(1)} %copy-done.1), custom_call_target="tpu_custom_call" | custom-call | flops 10000000000 | bytes 1000000 | tf_op jit(solution)/shard_map/pallas_call | solution.py:333
  11.9 0.0 collective-permute-done.5
  11.9 4.4 %collective-permute-done.4 = f32[4,40,128]{2,1,0:T(8,128)S(1)} collective-permute-done((f32[4,40,128]{2,1,0:T(8,128)S(1)}, f32[4,40,128]{2,1,0:T(8,128)S(1)}, u32[]{:S(2)}, u32[]{:S(2)}) %collective-permute-start.4) | collective-permute-done | bytes 81952 | tf_op jit(solution)/shard_map/ppermute | solution.py:327
  16.4 0.0 collective-permute-done.3
  16.4 1.2 %collective-permute-start.6 = (f32[16,40,128]{2,1,0:T(8,128)S(1)}, f32[16,40,128]{2,1,0:T(8,128)S(1)}, u32[]{:S(2)}, u32[]{:S(2)}) collective-permute-start(f32[16,40,128]{2,1,0:T(8,128)S(1)} %pad_maximum_fusion.mine_ref), channel_id=1, source_target_pairs={{0,1},{1,0},{2,3},{3,2},{4,5},{5,4},{6,7},{7,6},{8,9},{9,8},{10,11... | collective-permute-start | bytes 983048 | tf_op jit(solution)/shard_map/ppermute | solution.py:327
  17.6 0.0 copy-start
  17.6 0.1 pad_add_fusion.self_ref
  17.7 1.2 %collective-permute-done.6.twin_ref = f32[16,40,128]{2,1,0:T(8,128)S(1)} collective-permute-done((f32[16,40,128]{2,1,0:T(8,128)S(1)}, f32[16,40,128]{2,1,0:T(8,128)S(1)}, u32[]{:S(2)}, u32[]{:S(2)}) %collective-permute-start.6) | collective-permute-done | bytes 327712 | tf_op jit(solution)/shard_map/ppermute | solution.py:327
  18.9 0.0 copy-start.2
  18.9 0.0 copy-done
  18.9 0.7 %copy-done.2 = s32[16]{0:T(128)S(1)} copy-done((s32[16]{0:T(128)S(1)}, s32[16]{0:T(128)}, u32[]{:S(2)}) %copy-start.2) | copy-done | bytes 88
  19.5 19.3 %shard_map.56 = f32[3,2048]{1,0:T(4,128)} custom-call(s32[16,16]{1,0:T(8,128)S(1)} %copy-done, s32[16]{0:T(128)S(1)} %copy-done.2, s32[2]{0:T(128)S(1)} %pad_add_fusion.self_ref, f32[3,16,128]{2,1,0:T(8,128)S(1)} %get-tuple-element.13.tiled_ref, f32[3,128]{1,0:T(4,128)S(1)} %get-tuple-element.16.origin_ref, ...), custom_call_target="tpu_custom_call" | custom-call | tf_op jit(solution)/shard_map/pallas_call | solution.py:353
  (5 shorter events, 0.0 us)
Async XLA Ops:
  0.0 3.4 %collective-permute-start = (f32[10,512]{1,0:T(8,128)}, f32[10,512]{1,0:T(8,128)S(1)}, u32[]{:S(2)}, u32[]{:S(2)}) collective-permute-start(f32[10,512]{1,0:T(8,128)} %param.6), channel_id=1, source_target_pairs={{0,8},{8,0},{16,24},{24,16},{1,9},{9,1},{17,25},{25,17},{2,10},{10... | collective-permute-start | bytes 61448 | tf_op jit(solution)/shard_map/ppermute | solution.py:327
  0.0 4.3 %collective-permute-start.2 = (f32[10,512]{1,0:T(8,128)}, f32[10,512]{1,0:T(8,128)S(1)}, u32[]{:S(2)}, u32[]{:S(2)}) collective-permute-start(f32[10,512]{1,0:T(8,128)} %param.6), channel_id=1, source_target_pairs={{0,24},{8,16},{16,8},{24,0},{1,25},{9,17},{17,9},{25,1},{2,26},{10... | collective-permute-start | bytes 61448 | tf_op jit(solution)/shard_map/ppermute | solution.py:327
  2.4 3.3 %collective-permute-start.1 = (f32[10,512]{1,0:T(8,128)}, f32[10,512]{1,0:T(8,128)S(1)}, u32[]{:S(2)}, u32[]{:S(2)}) collective-permute-start(f32[10,512]{1,0:T(8,128)} %param.6), channel_id=1, source_target_pairs={{0,16},{8,24},{16,0},{24,8},{1,17},{9,25},{17,1},{25,9},{2,18},{10... | collective-permute-start | bytes 61448 | tf_op jit(solution)/shard_map/ppermute | solution.py:327
  5.8 3.9 %copy-start.1 = (s32[1,2048]{1,0:T(1,128)S(1)}, s32[1,2048]{1,0:T(1,128)}, u32[]{:S(2)}) copy-start(s32[1,2048]{1,0:T(1,128)} %slot_ref.3) | copy-start | bytes 24580
  5.8 3.9 %copy-start.3 = (f32[3,2048]{1,0:T(4,128)S(1)}, f32[3,2048]{1,0:T(4,128)}, u32[]{:S(2)}) copy-start(f32[3,2048]{1,0:T(4,128)} %pos_ref) | copy-start | bytes 73732
  5.8 6.1 %collective-permute-start.5 = (f32[4,40,128]{2,1,0:T(8,128)S(1)}, f32[4,40,128]{2,1,0:T(8,128)S(1)}, u32[]{:S(2)}, u32[]{:S(2)}) collective-permute-start(f32[4,40,128]{2,1,0:T(8,128)S(1)} %pad_maximum_fusion.1), channel_id=1, source_target_pairs={{0,6},{1,7},{2,4},{3,5},{4,2},{5,3},{6,0},{7,1},{8,14},{9,15},{10,... | collective-permute-start | bytes 245768 | tf_op jit(solution)/shard_map/ppermute | solution.py:327
  9.3 7.1 %collective-permute-start.4 = (f32[4,40,128]{2,1,0:T(8,128)S(1)}, f32[4,40,128]{2,1,0:T(8,128)S(1)}, u32[]{:S(2)}, u32[]{:S(2)}) collective-permute-start(f32[4,40,128]{2,1,0:T(8,128)S(1)} %pad_maximum_fusion.1), channel_id=1, source_target_pairs={{0,4},{1,5},{2,6},{3,7},{4,0},{5,1},{6,2},{7,3},{8,12},{9,13},{10,... | collective-permute-start | bytes 245768 | tf_op jit(solution)/shard_map/ppermute | solution.py:327
  9.3 7.1 %collective-permute-start.3 = (f32[4,40,128]{2,1,0:T(8,128)S(1)}, f32[4,40,128]{2,1,0:T(8,128)S(1)}, u32[]{:S(2)}, u32[]{:S(2)}) collective-permute-start(f32[4,40,128]{2,1,0:T(8,128)S(1)} %pad_maximum_fusion.1), channel_id=1, source_target_pairs={{0,2},{1,3},{2,0},{3,1},{4,6},{5,7},{6,4},{7,5},{8,10},{9,11},{10,... | collective-permute-start | bytes 245768 | tf_op jit(solution)/shard_map/ppermute | solution.py:327
  16.4 2.5 %collective-permute-start.6 = (f32[16,40,128]{2,1,0:T(8,128)S(1)}, f32[16,40,128]{2,1,0:T(8,128)S(1)}, u32[]{:S(2)}, u32[]{:S(2)}) collective-permute-start(f32[16,40,128]{2,1,0:T(8,128)S(1)} %pad_maximum_fusion.mine_ref), channel_id=1, source_target_pairs={{0,1},{1,0},{2,3},{3,2},{4,5},{5,4},{6,7},{7,6},{8,9},{9,8},{10,11... | collective-permute-start | bytes 983048 | tf_op jit(solution)/shard_map/ppermute | solution.py:327
  17.6 1.3 %copy-start = (s32[16,16]{1,0:T(8,128)S(1)}, s32[16,16]{1,0:T(8,128)}, u32[]{:S(2)}) copy-start(s32[16,16]{1,0:T(8,128)} %lists_ref.1) | copy-start | bytes 3076
  18.9 0.7 %copy-start.2 = (s32[16]{0:T(128)S(1)}, s32[16]{0:T(128)}, u32[]{:S(2)}) copy-start(s32[16]{0:T(128)} %counts_ref.1) | copy-start | bytes 196

commit v2 on v0

--- a/solution.py
+++ b/solution.py
@@ -8,11 +8,13 @@
 from jax.experimental.pallas import tpu as pltpu
 from jax.sharding import PartitionSpec as P
 
+
 LANES = 128
 SUBS = 8
 PAIRS = 8
 FEATURES = 48
 WEIGHTS = 40
+BLOCK_ROOM = 2**16
 split_a = 0.5
 soft_sq = 0.25
 root_pi = math.sqrt(math.pi)
@@ -62,27 +64,70 @@
     return rows == lax.shift_right_logical(slots, 7)
 
 
-def prep_kernel(pos_ref, slot_ref, tiled_ref, origin_ref, left_ref, rows_ref):
+def prep_kernel(
+    gx,
+    gy,
+    each,
+    self_ref,
+    lists_hbm,
+    counts_hbm,
+    pos_hbm,
+    slot_hbm,
+    nodes_hbm,
+    tiled_ref,
+    origin_ref,
+    left_ref,
+    near_list_ref,
+    far_list_ref,
+    own_ref,
+    rows_ref,
+    lists_ref,
+    counts_ref,
+    pos_ref,
+    slot_ref,
+    nodes_ref,
+    sems,
+):
     count = pos_ref.shape[1]
     tiles = count // LANES
+    moves = (
+        (pos_hbm, pos_ref),
+        (slot_hbm, slot_ref),
+        (lists_hbm, lists_ref),
+        (counts_hbm, counts_ref),
+        (nodes_hbm, nodes_ref),
+    )
+    copies = [
+        pltpu.make_async_copy(source, target, sems.at[i])
+        for i, (source, target) in enumerate(moves)
+    ]
+    for copy in copies:
+        copy.start()
+    for copy in copies:
+        copy.wait()
+    for j in range(each):
+        own_ref[pl.ds(j, 10, stride=each), :] = nodes_ref[:, j * LANES : (j + 1) * LANES]
     slots = slot_ref[...]
     owner = owners(slots, tiles, count)
     hot = hot_lanes(slots, count)
-    place = []
+    rows = []
     for c in range(3):
         value = pos_ref[c : c + 1, :]
         origin = jnp.sum(value, axis=1, keepdims=True) * (1.0 / count)
         origin_ref[c : c + 1, :] = jnp.broadcast_to(origin, (1, LANES))
-        value = value - origin
-        total = None
-        for part in thirds(value):
-            rows = jnp.where(owner, part, 0.0).astype(jnp.bfloat16)
-            got = lax.dot_general(
-                rows, hot, (((1,), (1,)), ((), ())), preferred_element_type=jnp.float32
-            )
-            total = got if total is None else total + got
-        tiled_ref[c] = total
-        place.append(total)
+        for part in thirds(value - origin):
+            rows.append(jnp.where(owner, part, 0.0).astype(jnp.bfloat16))
+    got = lax.dot_general(
+        jnp.concatenate(rows, axis=0),
+        hot,
+        (((1,), (1,)), ((), ())),
+        preferred_element_type=jnp.float32,
+    )
+    place = []
+    for c in range(3):
+        top, mid, low = (got[(3 * c + p) * tiles : (3 * c + p + 1) * tiles, :] for p in range(3))
+        tiled_ref[c] = top + mid + low
+        place.append(top + mid + low)
     x, y, z = place
     one = jnp.ones_like(x)
     zero = jnp.zeros_like(x)
@@ -97,8 +142,57 @@
     for t in range(tiles):
         left_ref[t] = rows_ref[pl.ds(t * LANES, LANES), :].T.astype(jnp.bfloat16)
 
-
-def node_features(origin_ref, nodes_ref, feats_ref, weights_ref):
+    block = lists_ref[...]
+    length = block.shape[1]
+    dev = quotient(block, each)
+    far_x = quotient(dev, gy) ^ self_ref[0]
+    far_y = (dev & (gy - 1)) ^ self_ref[1]
+    core, far_z = far_y & 1, lax.shift_right_logical(far_y, 1)
+    inside = block & (each - 1)
+    near_at = (core * gx + far_x) * each + inside
+    far_at = ((core * (gy // 2 - 1) + far_z - 1) * gx + far_x) * each + inside
+    tile_of = lax.broadcasted_iota(jnp.int32, (tiles, length), 0)
+    slot = lax.broadcasted_iota(jnp.int32, (tiles, length), 1)
+    limit = jnp.zeros((tiles, length), jnp.int32)
+    for t in range(tiles):
+        limit = jnp.where(tile_of == t, counts_ref[t], limit)
+    live = slot < limit
+    before = lax.broadcasted_iota(jnp.int32, (length, length), 0)
+    before = before < lax.broadcasted_iota(jnp.int32, (length, length), 1)
+    above = lax.broadcasted_iota(jnp.int32, (tiles, tiles), 1)
+    above = above < lax.broadcasted_iota(jnp.int32, (tiles, tiles), 0)
+    for out_ref, member, at in (
+        (near_list_ref, far_z == 0, near_at),
+        (far_list_ref, far_z != 0, far_at),
+    ):
+        member = live & member
+        hits = jnp.where(member, 1.0, 0.0)
+        number = jnp.sum(hits, axis=1, keepdims=True)
+        ahead = jnp.dot(
+            hits.astype(jnp.bfloat16),
+            jnp.where(before, 1.0, 0.0).astype(jnp.bfloat16),
+            preferred_element_type=jnp.float32,
+        )
+        ahead += jnp.dot(
+            jnp.where(above, 1.0, 0.0).astype(jnp.bfloat16),
+            jnp.broadcast_to(number, (tiles, length)).astype(jnp.bfloat16),
+            preferred_element_type=jnp.float32,
+        )
+        ahead = jnp.where(member, ahead, -1.0)
+        room = out_ref.shape[1]
+        entry = tile_of * BLOCK_ROOM + at - tiles * BLOCK_ROOM
+        where = lax.broadcasted_iota(jnp.int32, (tiles, room), 1)
+        total = jnp.zeros((tiles, room), jnp.int32)
+        for k in range(length):
+            mine = ahead[:, k : k + 1].astype(jnp.int32)
+            total += jnp.where(where == mine, entry[:, k : k + 1], 0)
+        total = jnp.sum(total, axis=0, keepdims=True) + tiles * BLOCK_ROOM
+        last = lax.broadcasted_iota(jnp.int32, (1, room), 1) == room - 1
+        total = jnp.where(last, jnp.sum(number).astype(jnp.int32), total)
+        out_ref[...] = total
+
+
+def node_features(origin_ref, nodes_ref, feats_ref, weights_ref, start):
     devices, rows, _ = nodes_ref.shape
     each = rows // 10
     group = max(1, SUBS // each)
@@ -114,7 +208,7 @@
             return parts[0] if group == 1 else jnp.concatenate(parts, axis=0)
 
         def put(ref, high, r, value):
-            ref[pl.ds(i * (wide * high) + r, wide, stride=high), :] = value
+            ref[pl.ds((start + i * wide) * high + r * wide, wide), :] = value
 
         mass = row(0)
         cx, cy, cz = (row(1 + c) - centre[c] for c in range(3))
@@ -159,14 +253,18 @@
     lax.fori_loop(0, devices // group, some, 0)
 
 
-def distances(left, feats_ref, block, near_ref):
-    base = pl.multiple_of(block * FEATURES, SUBS)
+def rows_of(ref, high, wide, block, first, number):
+    base = quotient(block, wide) * (high * wide) + (block & (wide - 1))
+    return ref[pl.ds(base + first * wide, number, stride=wide), :]
+
+
+def distances(left, take, near_ref):
     rows = lax.broadcasted_iota(jnp.int32, (SUBS, LANES), 0)
     zero = jnp.zeros((SUBS, LANES), jnp.float32)
     first, second = [], []
     for s in range(3):
-        one = feats_ref[pl.ds(base + s * 16, SUBS), :]
-        two = feats_ref[pl.ds(base + s * 16 + SUBS, SUBS), :]
+        one = take(s * 16, SUBS)
+        two = take(s * 16 + SUBS, SUBS)
         first.append(jnp.concatenate([jnp.where(rows < 5, one, 0.0), zero], axis=0))
         second.append(
             jnp.concatenate(
@@ -181,8 +279,7 @@
     near_ref[...] = jnp.dot(left, right, preferred_element_type=jnp.float32)
 
 
-def pair_terms(near_ref, feats_ref, block, terms_ref):
-    mass = feats_ref[pl.ds(block * FEATURES + 15, 1), :]
+def pair_terms(near_ref, mass, terms_ref):
     step = 2 * SUBS
     for g in range(LANES // step):
         at = pl.ds(g * step, step)
@@ -206,12 +303,9 @@
             terms_ref[2 + i, at, :] = low
 
 
-def add_forces(terms_ref, weights_ref, block, total_ref, tile):
-    base = pl.multiple_of(block * WEIGHTS, SUBS)
-    top = jnp.concatenate(
-        [weights_ref[pl.ds(base, 16), :], jnp.zeros((SUBS, LANES), jnp.float32)], axis=0
-    )
-    low = weights_ref[pl.ds(base + 16, 24), :]
+def add_forces(terms_ref, take, total_ref, tile):
+    top = jnp.concatenate([take(0, 16), jnp.zeros((SUBS, LANES), jnp.float32)], axis=0)
+    low = take(16, 24)
     right = jnp.concatenate([top, low, top, low], axis=1).astype(jnp.bfloat16)
     left = jnp.concatenate([terms_ref[i] for i in range(4)], axis=1)
     got = lax.dot_general(
@@ -220,75 +314,79 @@
     total_ref[tile, :, 0:24] += got
 
 
-def main_kernel(
-    gx,
-    gy,
-    lists_ref,
-    counts_ref,
+def all_pairs(list_ref, origin_ref, left_ref, mine_ref, twin_ref, total_ref, scratch):
+    feats_ref, weights_ref, near_ref, terms_ref = scratch
+    tiles = left_ref.shape[0]
+    each = mine_ref.shape[1] // 10
+    wide = max(1, SUBS // each) * each
+    half = mine_ref.shape[0] * each
+    node_features(origin_ref, mine_ref, feats_ref, weights_ref, 0)
+    node_features(origin_ref, twin_ref, feats_ref, weights_ref, half)
+
+    def ahead(u, n):
+        entry = list_ref[0, n]
+        tile, block = quotient(entry, BLOCK_ROOM), entry & (BLOCK_ROOM - 1)
+        take = functools.partial(rows_of, feats_ref, FEATURES, wide, block)
+        distances(left_ref[jnp.minimum(tile, tiles - 1)], take, near_ref.at[u])
+        return tile, block
+
+    def behind(u, pair):
+        take = functools.partial(rows_of, weights_ref, WEIGHTS, wide, pair[1])
+        add_forces(terms_ref.at[u], take, total_ref, pair[0])
+
+    def step(i, carry):
+        pairs, last = carry
+        nexts = []
+        behind(PAIRS - 1, last)
+        for u in range(PAIRS):
+            mass = rows_of(feats_ref, FEATURES, wide, pairs[u][1], 15, 1)
+            pair_terms(near_ref.at[u], mass, terms_ref.at[u])
+            nexts.append(ahead(u, (i + 1) * PAIRS + u))
+            if u + 1 < PAIRS:
+                behind(u, pairs[u])
+        return tuple(nexts), pairs[-1]
+
+    pairs = tuple(ahead(u, u) for u in range(PAIRS))
+    none = (jnp.int32(tiles), jnp.int32(0))
+    terms_ref[PAIRS - 1] = jnp.zeros(terms_ref.shape[1:], terms_ref.dtype)
+    live = list_ref[0, list_ref.shape[1] - 1]
+    steps = quotient(live + (PAIRS - 1), PAIRS)
+    carry = lax.fori_loop(0, steps, step, (pairs, none))
+    behind(PAIRS - 1, carry[-1])
+
+
+def near_kernel(list_ref, origin_ref, left_ref, mine_ref, twin_ref, total_ref, *scratch):
+    total_ref[...] = jnp.zeros_like(total_ref)
+    all_pairs(list_ref, origin_ref, left_ref, mine_ref, twin_ref, total_ref, scratch)
+
+
+def far_kernel(
+    list_ref,
     tiled_ref,
     origin_ref,
     left_ref,
     slot_ref,
-    nodes_ref,
+    mine_ref,
+    twin_ref,
+    start_ref,
     out_ref,
-    feats_ref,
-    weights_ref,
-    near_ref,
-    terms_ref,
     total_ref,
     flat_ref,
+    *scratch,
 ):
     count = slot_ref.shape[1]
     tiles = count // LANES
-    each = nodes_ref.shape[1] // 10
-    node_features(origin_ref, nodes_ref, feats_ref, weights_ref)
-    total_ref[...] = jnp.zeros_like(total_ref)
-    live = lax.fori_loop(0, tiles, lambda t, n: n + counts_ref[t], 0)
-
-    def take(t, k):
-        row = jnp.minimum(t, tiles - 1)
-        block = lists_ref[row, k]
-        dev = quotient(block, each)
-        place = (dev % gy) * gx + quotient(dev, gy)
-        block = place * each + block % each
-        wrap = k + 1 >= counts_ref[row]
-        return row, jnp.minimum(t, tiles), block, jnp.where(wrap, t + 1, t), jnp.where(wrap, 0, k + 1)
-
-    def ahead(u, t, k):
-        row, tile, block, t, k = take(t, k)
-        distances(left_ref[row], feats_ref, block, near_ref.at[u])
-        return (tile, block), t, k
-
-    def behind(u, pair):
-        add_forces(terms_ref.at[u], weights_ref, pair[1], total_ref, pair[0])
-
-    def step(i, carry):
-        t, k, pairs, last = carry
-        nexts = []
-        behind(PAIRS - 1, last)
-        for u in range(PAIRS):
-            pair_terms(near_ref.at[u], feats_ref, pairs[u][1], terms_ref.at[u])
-            pair, t, k = ahead(u, t, k)
-            nexts.append(pair)
-            if u + 1 < PAIRS:
-                behind(u, pairs[u])
-        return t, k, tuple(nexts), pairs[-1]
-
-    t, k, pairs = jnp.int32(0), jnp.int32(0), []
-    for u in range(PAIRS):
-        pair, t, k = ahead(u, t, k)
-        pairs.append(pair)
-    none = (jnp.int32(tiles), jnp.int32(0))
-    terms_ref[PAIRS - 1] = jnp.zeros(terms_ref.shape[1:], terms_ref.dtype)
-    steps = lax.div(live + (PAIRS - 1), PAIRS)
-    carry = lax.fori_loop(0, steps, step, (t, k, tuple(pairs), none))
-    behind(PAIRS - 1, carry[-1])
-
-    for t in range(tiles):
-        flat_ref[pl.ds(t * LANES, LANES), :] = total_ref[t].T
+    total_ref[...] = start_ref[...]
+    all_pairs(list_ref, origin_ref, left_ref, mine_ref, twin_ref, total_ref, scratch)
+    room = LANES // 4
+    for q in range(0, tiles, 4):
+        four = total_ref[q]
+        for j in range(1, min(4, tiles - q)):
+            four += pltpu.roll(total_ref[q + j], room * j, 1)
+        flat_ref[pl.ds(q * room, LANES), :] = four.T
 
     def column(r):
-        return flat_ref[pl.ds(r, tiles, stride=LANES), :]
+        return flat_ref[pl.ds(r, tiles, stride=room), :]
 
     x, y, z = tiled_ref[0], tiled_ref[1], tiled_ref[2]
     sums = column(9)
@@ -301,51 +399,106 @@
     ]
     slots = slot_ref[...]
     owner = owners(slots, tiles, count)
-    hot = hot_lanes(slots, count)
+    parts = [part.astype(jnp.bfloat16) for force in forces for part in thirds(force)]
+    got = jnp.dot(
+        jnp.concatenate(parts, axis=0),
+        hot_lanes(slots, count),
+        preferred_element_type=jnp.float32,
+    )
     for c in range(3):
-        total = None
-        for part in thirds(forces[c]):
-            got = jnp.dot(part.astype(jnp.bfloat16), hot, preferred_element_type=jnp.float32)
-            total = got if total is None else total + got
-        out_ref[c : c + 1, :] = jnp.sum(jnp.where(owner, total, 0.0), axis=0, keepdims=True)
+        top, mid, low = (got[(3 * c + p) * tiles : (3 * c + p + 1) * tiles, :] for p in range(3))
+        chosen = jnp.where(owner, top + mid + low, 0.0)
+        out_ref[c : c + 1, :] = jnp.sum(chosen, axis=0, keepdims=True)
+
+
+def estimate(flops):
+    return pl.CostEstimate(flops=flops, bytes_accessed=10**6, transcendentals=0)
 
 
 def shards(gx, gy, positions, node_moments, slot_of, block_list, tile_counts):
     count = positions.shape[1]
     tiles = count // LANES
     each = node_moments.shape[1] // LANES
-    blocks = each * gx * gy
-    packed = node_moments.reshape(10 * each, LANES)
+    room = pl.cdiv(block_list.size + 2 * PAIRS + 1, LANES) * LANES
     vmem = pl.BlockSpec(memory_space=pltpu.VMEM)
     smem = pl.BlockSpec(memory_space=pltpu.SMEM)
-    tiled, origin, left = pl.pallas_call(
-        prep_kernel,
+
+    def swap(value, axis, size, bits):
+        return lax.ppermute(value, axis, [(i, i ^ bits) for i in range(size)])
+
+    def work(blocks):
+        shapes = [
+            pltpu.VMEM((blocks * FEATURES, LANES), jnp.float32),
+            pltpu.VMEM((blocks * WEIGHTS, LANES), jnp.float32),
+            pltpu.VMEM((PAIRS, LANES, 2 * LANES), jnp.float32),
+            pltpu.VMEM((PAIRS, 4, LANES, LANES), jnp.bfloat16),
+        ]
+        rows = blocks * (FEATURES + WEIGHTS) + PAIRS * 4 * LANES + tiles * 2 * LANES
+        limit = min(rows * 4 * LANES + 2**21, 60 * 1024 * 1024)
+        return shapes, pltpu.CompilerParams(vmem_limit_bytes=limit)
+
+    here = jnp.stack([lax.axis_index("gx"), lax.axis_index("gy")]).astype(jnp.int32)
+    prepare = pl.pallas_call(
+        functools.partial(prep_kernel, gx, gy, each),
         out_shape=(
             jax.ShapeDtypeStruct((3, tiles, LANES), jnp.float32),
             jax.ShapeDtypeStruct((3, LANES), jnp.float32),
             jax.ShapeDtypeStruct((tiles, LANES, LANES), jnp.bfloat16),
+            jax.ShapeDtypeStruct((1, room), jnp.int32),
+            jax.ShapeDtypeStruct((1, room), jnp.int32),
+            jax.ShapeDtypeStruct((10 * each, LANES), jnp.float32),
         ),
-        in_specs=[vmem] * 2,
-        out_specs=(vmem,) * 3,
-        scratch_shapes=[pltpu.VMEM((tiles * LANES, LANES), jnp.float32)],
-    )(positions, slot_of)
-    every = lax.all_gather(packed, "gx", axis=0)
-    every = lax.all_gather(every, "gy", axis=0)
-    every = every.reshape(gx * gy, 10 * each, LANES)
+        in_specs=[smem] + [pl.BlockSpec(memory_space=pltpu.HBM)] * 5,
+        out_specs=(vmem,) * 6,
+        scratch_shapes=[
+            pltpu.VMEM((tiles * LANES, LANES), jnp.float32),
+            pltpu.VMEM(block_list.shape, jnp.int32),
+            pltpu.SMEM(tile_counts.shape, jnp.int32),
+            pltpu.VMEM(positions.shape, jnp.float32),
+            pltpu.VMEM(slot_of.shape, jnp.int32),
+            pltpu.VMEM(node_moments.shape, jnp.float32),
+            pltpu.SemaphoreType.DMA((5,)),
+        ],
+        compiler_params=pltpu.CompilerParams(vmem_limit_bytes=8 * 2**20),
+        cost_estimate=estimate(10**10),
+    )
+    held = [
+        pltpu.with_memory_space_constraint(value, pltpu.HBM)
+        for value in (block_list, tile_counts, positions, slot_of, node_moments)
+    ]
+    tiled, origin, left, near_list, far_list, own = prepare(here, *held)
+    near = [swap(node_moments, "gx", gx, b) for b in range(1, gx)]
+    near = jnp.stack([own] + [value.reshape(10 * each, LANES) for value in near])
+    near, origin = lax.optimization_barrier((near, origin))
+    far = [swap(near, "gy", gy, b) for b in range(2, gy, 2)]
+    near_twin = swap(near, "gy", gy, 1)
+    near_work, near_params = work(2 * gx * each)
+    near_pairs = pl.pallas_call(
+        near_kernel,
+        out_shape=jax.ShapeDtypeStruct((tiles + 1, LANES, LANES), jnp.float32),
+        in_specs=[smem] + [vmem] * 4,
+        out_specs=vmem,
+        scratch_shapes=near_work,
+        compiler_params=near_params,
+        cost_estimate=estimate(10**10),
+    )
+    total = near_pairs(near_list, origin, left, near, near_twin)
+    far = jnp.concatenate(far, axis=0)
+    far, total = lax.optimization_barrier((far, total))
+    far_twin = swap(far, "gy", gy, 1)
+    far_work, far_params = work((gy - 2) * gx * each)
     return pl.pallas_call(
-        functools.partial(main_kernel, gx, gy),
+        far_kernel,
         out_shape=jax.ShapeDtypeStruct((3, count), jnp.float32),
-        in_specs=[smem] * 2 + [vmem] * 5,
+        in_specs=[smem] + [vmem] * 7,
         out_specs=vmem,
         scratch_shapes=[
-            pltpu.VMEM((blocks * FEATURES, LANES), jnp.float32),
-            pltpu.VMEM((blocks * WEIGHTS, LANES), jnp.float32),
-            pltpu.VMEM((PAIRS, LANES, 2 * LANES), jnp.float32),
-            pltpu.VMEM((PAIRS, 4, LANES, LANES), jnp.bfloat16),
             pltpu.VMEM((tiles + 1, LANES, LANES), jnp.float32),
-            pltpu.VMEM((tiles * LANES, LANES), jnp.float32),
-        ],
-    )(block_list, tile_counts, tiled, origin, left, slot_of, every)
+            pltpu.VMEM((pl.cdiv(tiles, 4) * LANES, LANES), jnp.float32),
+        ]
+        + far_work,
+        compiler_params=far_params,
+    )(far_list, tiled, origin, left, slot_of, far, far_twin, total)
 
 
 def solution(mesh):
@@ -356,10 +509,10 @@
         P(("gx", "gy"), None),
         P(("gx", "gy")),
     )
+
+    def body(*args):
+        return shards(mesh.shape["gx"], mesh.shape["gy"], *args)
+
     return jax.shard_map(
-        functools.partial(shards, mesh.shape["gx"], mesh.shape["gy"]),
-        mesh=mesh,
-        in_specs=placed,
-        out_specs=P(None, ("gx", "gy")),
-        check_vma=False,
-    )
+        body, mesh=mesh, in_specs=placed, out_specs=P(None, ("gx", "gy")), check_vma=False
+    )

time: 52.1 us -> 38.1 us (0.73)
  the two profiles are of different devices: /device:TPU:13 before, /device:TPU:15 now
where the time goes in v2:
time: 38.1 us; the launch traced here: 37.9 us
  Pallas kernels  23.3 us (61%)
  starting transfers between devices  10.7 us (28%)
  waiting for transfers between devices  3.69 us (10%)
    pallas_call x1, Pallas kernels, shards(): pl.pallas_call(far_kernel, out_shape=jax.ShapeDtypeStruct((3, count), jnp...  14.6 us
    ppermute x8, starting transfers between devices, swap(): return lax.ppermute(value, axis, [(i, i ^ bits) for i in range(size)])  10.7 us
    pallas_call x1, Pallas kernels, shards(): total = near_pairs(near_list, origin, left, near, near_twin)  5.77 us
    ppermute x8, waiting for transfers between devices, swap(): return lax.ppermute(value, axis, [(i, i ^ bits) for i in range(size)])  3.69 us
    pallas_call x1, Pallas kernels, shards(): tiled, origin, left, near_list, far_list, own = prepare(here, *held)  2.99 us
  transfers between devices with their start and end apart: 8, of which 3 were waited for; matrix products, arithmetic and copies ran while one was open for 0% of the time, Pallas kernels for 8%

profile of v2, /device:TPU:15, one launch (start us, length us, event | category | flops | bytes accessed | tf_op | source)
XLA Modules:
  0.0 37.9 jit_solution(15650142163913763616)
XLA Ops:
  0.0 0.3 collective-permute-start
  0.3 1.2 %collective-permute-start.2 = (f32[10,512]{1,0:T(8,128)}, f32[10,512]{1,0:T(8,128)S(1)}, u32[]{:S(2)}, u32[]{:S(2)}) collective-permute-start(f32[10,512]{1,0:T(8,128)} %nodes_hbm.1), channel_id=1, source_target_pairs={{0,24},{8,16},{16,8},{24,0},{1,25},{9,17},{17,9},{25,1},{2,26},{10... | collective-permute-start | bytes 61448 | tf_op jit(solution)/shard_map/ppermute | solution.py:427
  1.4 1.2 %collective-permute-start.1 = (f32[10,512]{1,0:T(8,128)}, f32[10,512]{1,0:T(8,128)S(1)}, u32[]{:S(2)}, u32[]{:S(2)}) collective-permute-start(f32[10,512]{1,0:T(8,128)} %nodes_hbm.1), channel_id=1, source_target_pairs={{0,16},{8,24},{16,0},{24,8},{1,17},{9,25},{17,1},{25,9},{2,18},{10... | collective-permute-start | bytes 61448 | tf_op jit(solution)/shard_map/ppermute | solution.py:427
  2.7 0.1 pad_add_fusion.self_ref
  2.7 3.0 %shard_map.55 = (f32[3,16,128]{2,1,0:T(8,128)S(1)}, f32[3,128]{1,0:T(4,128)S(1)}, bf16[16,128,128]{2,1,0:T(8,128)(2,1)S(1)}, s32[1,384]{1,0:T(1,128)S(1)}, s32[1,384]{1,0:T(1,128)S(1)}, /*index=5*/f32[40,128]{1,0:T(8,128)S(1)}) custom-call(s32[2]{0:T(128)S(1)} %pad_add_fusion.self_ref, s32[16,16]{1,0:T(8,128)} %lists_hbm.1, s32[16]{0:T(128)} %counts_hbm.1, ...), custom_call_target="tpu_custom_call" | custom-call | flops 10000000000 | bytes 1000000 | tf_op jit(solution)/shard_map/pallas_call | solution.py:469
  5.7 0.0 collective-permute-done
  5.7 0.0 collective-permute-done.2
  5.8 0.0 collective-permute-done.1
  5.8 1.4 %collective-permute-start.5 = (f32[4,40,128]{2,1,0:T(8,128)S(1)}, f32[4,40,128]{2,1,0:T(8,128)S(1)}, u32[]{:S(2)}, u32[]{:S(2)}) collective-permute-start(f32[4,40,128]{2,1,0:T(8,128)S(1)} %pad_maximum_fusion.1.mine_ref), channel_id=1, source_target_pairs={{0,6},{1,7},{2,4},{3,5},{4,2},{5,3},{6,0},{7,1},{8,14},{9,15},{10,... | collective-permute-start | bytes 245768 | tf_op jit(solution)/shard_map/ppermute | solution.py:427
  7.2 1.1 %collective-permute-start.4 = (f32[4,40,128]{2,1,0:T(8,128)S(1)}, f32[4,40,128]{2,1,0:T(8,128)S(1)}, u32[]{:S(2)}, u32[]{:S(2)}) collective-permute-start(f32[4,40,128]{2,1,0:T(8,128)S(1)} %pad_maximum_fusion.1.mine_ref), channel_id=1, source_target_pairs={{0,4},{1,5},{2,6},{3,7},{4,0},{5,1},{6,2},{7,3},{8,12},{9,13},{10,... | collective-permute-start | bytes 245768 | tf_op jit(solution)/shard_map/ppermute | solution.py:427
  8.3 1.1 %collective-permute-start.3 = (f32[4,40,128]{2,1,0:T(8,128)S(1)}, f32[4,40,128]{2,1,0:T(8,128)S(1)}, u32[]{:S(2)}, u32[]{:S(2)}) collective-permute-start(f32[4,40,128]{2,1,0:T(8,128)S(1)} %pad_maximum_fusion.1.mine_ref), channel_id=1, source_target_pairs={{0,2},{1,3},{2,0},{3,1},{4,6},{5,7},{6,4},{7,5},{8,10},{9,11},{10,... | collective-permute-start | bytes 245768 | tf_op jit(solution)/shard_map/ppermute | solution.py:427
  9.4 2.1 %collective-permute-start.6 = (f32[4,40,128]{2,1,0:T(8,128)S(1)}, f32[4,40,128]{2,1,0:T(8,128)S(1)}, u32[]{:S(2)}, u32[]{:S(2)}) collective-permute-start(f32[4,40,128]{2,1,0:T(8,128)S(1)} %pad_maximum_fusion.1.mine_ref), channel_id=1, source_target_pairs={{0,1},{1,0},{2,3},{3,2},{4,5},{5,4},{6,7},{7,6},{8,9},{9,8},{10,11... | collective-permute-start | bytes 245768 | tf_op jit(solution)/shard_map/ppermute | solution.py:427
  11.4 0.0 collective-permute-done.5
  11.4 0.2 collective-permute-done.4
  11.7 2.3 %collective-permute-done.3 = f32[4,40,128]{2,1,0:T(8,128)S(1)} collective-permute-done((f32[4,40,128]{2,1,0:T(8,128)S(1)}, f32[4,40,128]{2,1,0:T(8,128)S(1)}, u32[]{:S(2)}, u32[]{:S(2)}) %collective-permute-start.3) | collective-permute-done | bytes 81952 | tf_op jit(solution)/shard_map/ppermute | solution.py:427
  14.0 0.0 collective-permute-done.6.twin_ref
  14.0 0.0 copy-start
  14.0 5.8 %shard_map.56.start_ref = f32[17,128,128]{2,1,0:T(8,128)S(1)} custom-call(s32[1,384]{1,0:T(1,128)S(1)} %get-tuple-element.22.list_ref, f32[3,128]{1,0:T(4,128)S(1)} %get-tuple-element.19.origin_ref, bf16[16,128,128]{2,1,0:T(8,128)(2,1)S(1)} %get-tuple-element.20.left_ref, f32[4,40,128]{2,1,0:T(8,128)S(1)} %pad_maximum_fusion.1.mine_ref, ...), custom_call_target="tpu_custom_call" | custom-call | flops 10000000000 | bytes 1000000 | tf_op jit(solution)/shard_map/pallas_call | solution.py:485
  19.8 2.4 %collective-permute-start.7 = (f32[12,40,128]{2,1,0:T(8,128)S(1)}, f32[12,40,128]{2,1,0:T(8,128)S(1)}, u32[]{:S(2)}, u32[]{:S(2)}) collective-permute-start(f32[12,40,128]{2,1,0:T(8,128)S(1)} %pad_maximum_fusion.mine_ref), channel_id=1, source_target_pairs={{0,1},{1,0},{2,3},{3,2},{4,5},{5,4},{6,7},{7,6},{8,9},{9,8},{10,11... | collective-permute-start | bytes 737288 | tf_op jit(solution)/shard_map/ppermute | solution.py:427
  22.2 1.1 %collective-permute-done.7.twin_ref = f32[12,40,128]{2,1,0:T(8,128)S(1)} collective-permute-done((f32[12,40,128]{2,1,0:T(8,128)S(1)}, f32[12,40,128]{2,1,0:T(8,128)S(1)}, u32[]{:S(2)}, u32[]{:S(2)}) %collective-permute-start.7) | collective-permute-done | bytes 245792 | tf_op jit(solution)/shard_map/ppermute | solution.py:427
  23.3 0.0 copy-done
  23.4 14.6 %shard_map.57 = f32[3,2048]{1,0:T(4,128)} custom-call(s32[1,384]{1,0:T(1,128)S(1)} %get-tuple-element.15.list_ref, f32[3,16,128]{2,1,0:T(8,128)S(1)} %get-tuple-element.16.tiled_ref, f32[3,128]{1,0:T(4,128)S(1)} %get-tuple-element.19.origin_ref, bf16[16,128,128]{2,1,0:T(8,128)(2,1)S(1)} %get-tuple-element.20.left_ref, s32[1,2048]{1,0:T(1,128)S(1)} %copy-done, ...), custom_call_target="tpu_custom_call" | custom-call | tf_op jit(solution)/shard_map/pallas_call | solution.py:490
  (5 shorter events, 0.0 us)
Async XLA Ops:
  0.0 5.7 %collective-permute-start = (f32[10,512]{1,0:T(8,128)}, f32[10,512]{1,0:T(8,128)S(1)}, u32[]{:S(2)}, u32[]{:S(2)}) collective-permute-start(f32[10,512]{1,0:T(8,128)} %nodes_hbm.1), channel_id=1, source_target_pairs={{0,8},{8,0},{16,24},{24,16},{1,9},{9,1},{17,25},{25,17},{2,10},{10... | collective-permute-start | bytes 61448 | tf_op jit(solution)/shard_map/ppermute | solution.py:427
  0.3 5.5 %collective-permute-start.2 = (f32[10,512]{1,0:T(8,128)}, f32[10,512]{1,0:T(8,128)S(1)}, u32[]{:S(2)}, u32[]{:S(2)}) collective-permute-start(f32[10,512]{1,0:T(8,128)} %nodes_hbm.1), channel_id=1, source_target_pairs={{0,24},{8,16},{16,8},{24,0},{1,25},{9,17},{17,9},{25,1},{2,26},{10... | collective-permute-start | bytes 61448 | tf_op jit(solution)/shard_map/ppermute | solution.py:427
  1.4 4.4 %collective-permute-start.1 = (f32[10,512]{1,0:T(8,128)}, f32[10,512]{1,0:T(8,128)S(1)}, u32[]{:S(2)}, u32[]{:S(2)}) collective-permute-start(f32[10,512]{1,0:T(8,128)} %nodes_hbm.1), channel_id=1, source_target_pairs={{0,16},{8,24},{16,0},{24,8},{1,17},{9,25},{17,1},{25,9},{2,18},{10... | collective-permute-start | bytes 61448 | tf_op jit(solution)/shard_map/ppermute | solution.py:427
  5.8 5.6 %collective-permute-start.5 = (f32[4,40,128]{2,1,0:T(8,128)S(1)}, f32[4,40,128]{2,1,0:T(8,128)S(1)}, u32[]{:S(2)}, u32[]{:S(2)}) collective-permute-start(f32[4,40,128]{2,1,0:T(8,128)S(1)} %pad_maximum_fusion.1.mine_ref), channel_id=1, source_target_pairs={{0,6},{1,7},{2,4},{3,5},{4,2},{5,3},{6,0},{7,1},{8,14},{9,15},{10,... | collective-permute-start | bytes 245768 | tf_op jit(solution)/shard_map/ppermute | solution.py:427
  7.2 4.5 %collective-permute-start.4 = (f32[4,40,128]{2,1,0:T(8,128)S(1)}, f32[4,40,128]{2,1,0:T(8,128)S(1)}, u32[]{:S(2)}, u32[]{:S(2)}) collective-permute-start(f32[4,40,128]{2,1,0:T(8,128)S(1)} %pad_maximum_fusion.1.mine_ref), channel_id=1, source_target_pairs={{0,4},{1,5},{2,6},{3,7},{4,0},{5,1},{6,2},{7,3},{8,12},{9,13},{10,... | collective-permute-start | bytes 245768 | tf_op jit(solution)/shard_map/ppermute | solution.py:427
  8.3 5.7 %collective-permute-start.3 = (f32[4,40,128]{2,1,0:T(8,128)S(1)}, f32[4,40,128]{2,1,0:T(8,128)S(1)}, u32[]{:S(2)}, u32[]{:S(2)}) collective-permute-start(f32[4,40,128]{2,1,0:T(8,128)S(1)} %pad_maximum_fusion.1.mine_ref), channel_id=1, source_target_pairs={{0,2},{1,3},{2,0},{3,1},{4,6},{5,7},{6,4},{7,5},{8,10},{9,11},{10,... | collective-permute-start | bytes 245768 | tf_op jit(solution)/shard_map/ppermute | solution.py:427
  9.4 4.6 %collective-permute-start.6 = (f32[4,40,128]{2,1,0:T(8,128)S(1)}, f32[4,40,128]{2,1,0:T(8,128)S(1)}, u32[]{:S(2)}, u32[]{:S(2)}) collective-permute-start(f32[4,40,128]{2,1,0:T(8,128)S(1)} %pad_maximum_fusion.1.mine_ref), channel_id=1, source_target_pairs={{0,1},{1,0},{2,3},{3,2},{4,5},{5,4},{6,7},{7,6},{8,9},{9,8},{10,11... | collective-permute-start | bytes 245768 | tf_op jit(solution)/shard_map/ppermute | solution.py:427
  14.0 9.3 %copy-start = (s32[1,2048]{1,0:T(1,128)S(1)}, s32[1,2048]{1,0:T(1,128)}, u32[]{:S(2)}) copy-start(s32[1,2048]{1,0:T(1,128)} %slot_ref.1) | copy-start | bytes 24580
  19.8 3.5 %collective-permute-start.7 = (f32[12,40,128]{2,1,0:T(8,128)S(1)}, f32[12,40,128]{2,1,0:T(8,128)S(1)}, u32[]{:S(2)}, u32[]{:S(2)}) collective-permute-start(f32[12,40,128]{2,1,0:T(8,128)S(1)} %pad_maximum_fusion.mine_ref), channel_id=1, source_target_pairs={{0,1},{1,0},{2,3},{3,2},{4,5},{5,4},{6,7},{7,6},{8,9},{9,8},{10,11... | collective-permute-start | bytes 737288 | tf_op jit(solution)/shard_map/ppermute | solution.py:427

commit v3 on v2

--- a/solution.py
+++ b/solution.py
@@ -134,13 +134,13 @@
     terms = [x, y, z, one, -UNIT * (x * x + y * y + (z * z + soft_sq)), x, y, z]
     terms += [x * x, y * y, z * z, x * y, x * z, y * z, one, zero]
     for i, term in enumerate(terms):
-        top, mid, low = thirds(term)
-        for s, part in enumerate((top, top, top, mid, mid, low)):
-            rows_ref[pl.ds(s * 16 + i, tiles, stride=LANES), :] = part
-    for s in range(96, LANES):
-        rows_ref[pl.ds(s, tiles, stride=LANES), :] = zero
+        for s, part in enumerate(thirds(term)):
+            rows_ref[pl.ds(s * 16 + i, tiles, stride=FEATURES), :] = part
+    blank = jnp.zeros((LANES - 2 * FEATURES, LANES), jnp.float32)
     for t in range(tiles):
-        left_ref[t] = rows_ref[pl.ds(t * LANES, LANES), :].T.astype(jnp.bfloat16)
+        kind = [rows_ref[pl.ds(t * FEATURES + s * 16, 16), :] for s in range(3)]
+        rows = jnp.concatenate([kind[s] for s in (0, 0, 0, 1, 1, 2)] + [blank], axis=0)
+        left_ref[t] = rows.T.astype(jnp.bfloat16)
 
     block = lists_ref[...]
     length = block.shape[1]
@@ -218,7 +218,8 @@
         vz = qxz * cx + qyz * cy + qzz * cz
         terms = [2.0 * UNIT * cx, 2.0 * UNIT * cy, 2.0 * UNIT * cz]
         terms += [-UNIT * (cx * cx + cy * cy + cz * cz)]
-        one, two = 7.5 * UNIT**2, 15.0 * UNIT**2
+        one = (7.5 * UNIT**2) / mass
+        two = one + one
         terms += [jnp.ones(shape, jnp.float32), -two * vx, -two * vy, -two * vz]
         terms += [one * qxx, one * qyy, one * qzz, two * qxy, two * qxz, two * qyz]
         terms += [one * (vx * cx + vy * cy + vz * cz)]
@@ -226,28 +227,28 @@
             for s, part in enumerate(thirds(term)):
                 put(feats_ref, FEATURES, s * 16 + r, part)
         for s in range(3):
-            put(feats_ref, FEATURES, s * 16 + 15, mass)
+            put(feats_ref, FEATURES, s * 16 + 15, jnp.zeros(shape, jnp.float32))
         half = (1.5 * UNIT) * (qxx + qyy + qzz)
         full = 3.0 * UNIT
         diag = [full * qxx + half, full * qyy + half, full * qzz + half]
         near = [full * vx + half * cx, full * vy + half * cy, full * vz + half * cz]
         zero = jnp.zeros(shape, jnp.float32)
-        for c, value in enumerate((cx, cy, cz)):
+        for c, value in enumerate((mass * cx, mass * cy, mass * cz)):
             for s, part in enumerate(thirds(value)):
                 put(weights_ref, WEIGHTS, s * 3 + c, part)
-        put(weights_ref, WEIGHTS, 9, zero + 1.0)
-        for r in range(10, 16):
+        for s, part in enumerate(thirds(mass)):
+            put(weights_ref, WEIGHTS, 9 + s, part)
+        for r in range(12, 16):
             put(weights_ref, WEIGHTS, r, zero)
         for c, value in enumerate(near):
             for s, part in enumerate(thirds(value)):
                 put(weights_ref, WEIGHTS, 16 + s * 3 + c, -part)
-        put(weights_ref, WEIGHTS, 25, zero)
+        for r in range(25, 28):
+            put(weights_ref, WEIGHTS, r, zero)
         for c, value in enumerate(diag + [full * qxy, full * qxz, full * qyz]):
             top, mid, _ = thirds(value)
-            put(weights_ref, WEIGHTS, 26 + c, top)
-            put(weights_ref, WEIGHTS, 32 + c, mid)
-        put(weights_ref, WEIGHTS, 38, zero)
-        put(weights_ref, WEIGHTS, 39, zero)
+            put(weights_ref, WEIGHTS, 28 + c, top)
+            put(weights_ref, WEIGHTS, 34 + c, mid)
         return carry
 
     lax.fori_loop(0, devices // group, some, 0)
@@ -268,7 +269,7 @@
         first.append(jnp.concatenate([jnp.where(rows < 5, one, 0.0), zero], axis=0))
         second.append(
             jnp.concatenate(
-                [jnp.where(rows >= 5, one, 0.0), jnp.where(rows < 7, two, 0.0)], axis=0
+                [jnp.where(rows >= 5, one, 0.0), two], axis=0
             )
         )
     blank = jnp.zeros((LANES - 96, 2 * LANES), jnp.float32)
@@ -279,7 +280,7 @@
     near_ref[...] = jnp.dot(left, right, preferred_element_type=jnp.float32)
 
 
-def pair_terms(near_ref, mass, terms_ref):
+def pair_terms(near_ref, terms_ref):
     step = 2 * SUBS
     for g in range(LANES // step):
         at = pl.ds(g * step, step)
@@ -294,7 +295,7 @@
         first = poly * inv
         second = (first + ADD_2) * inv
         third = (second + ADD_3) * inv
-        radial = (mass * first + third * inner) * expo
+        radial = (first + third * inner) * expo
         second = second * expo
         for i, value in enumerate((radial, second)):
             top = value.astype(jnp.bfloat16)
@@ -306,12 +307,14 @@
 def add_forces(terms_ref, take, total_ref, tile):
     top = jnp.concatenate([take(0, 16), jnp.zeros((SUBS, LANES), jnp.float32)], axis=0)
     low = take(16, 24)
-    right = jnp.concatenate([top, low, top, low], axis=1).astype(jnp.bfloat16)
-    left = jnp.concatenate([terms_ref[i] for i in range(4)], axis=1)
+    right = jnp.concatenate([top, low], axis=1).astype(jnp.bfloat16)
+    left = jnp.concatenate(
+        [jnp.concatenate([terms_ref[i], terms_ref[i + 1]], axis=1) for i in (0, 2)], axis=0
+    )
     got = lax.dot_general(
         left, right, (((1,), (1,)), ((), ())), preferred_element_type=jnp.float32
     )
-    total_ref[tile, :, 0:24] += got
+    total_ref[tile, :, 0:24] += got[:LANES] + got[LANES:]
 
 
 def all_pairs(list_ref, origin_ref, left_ref, mine_ref, twin_ref, total_ref, scratch):
@@ -339,8 +342,7 @@
         nexts = []
         behind(PAIRS - 1, last)
         for u in range(PAIRS):
-            mass = rows_of(feats_ref, FEATURES, wide, pairs[u][1], 15, 1)
-            pair_terms(near_ref.at[u], mass, terms_ref.at[u])
+            pair_terms(near_ref.at[u], terms_ref.at[u])
             nexts.append(ahead(u, (i + 1) * PAIRS + u))
             if u + 1 < PAIRS:
                 behind(u, pairs[u])
@@ -389,8 +391,8 @@
         return flat_ref[pl.ds(r, tiles, stride=room), :]
 
     x, y, z = tiled_ref[0], tiled_ref[1], tiled_ref[2]
-    sums = column(9)
-    mxx, myy, mzz, mxy, mxz, myz = (column(10 + c) + column(16 + c) for c in range(6))
+    sums = column(9) + column(10) + column(11)
+    mxx, myy, mzz, mxy, mxz, myz = (column(12 + c) + column(18 + c) for c in range(6))
     const = [column(c) + column(3 + c) + column(6 + c) for c in range(3)]
     forces = [
         SCALE * (const[0] - x * sums + (mxx * x + mxy * y + mxz * z)),
@@ -451,7 +453,7 @@
         in_specs=[smem] + [pl.BlockSpec(memory_space=pltpu.HBM)] * 5,
         out_specs=(vmem,) * 6,
         scratch_shapes=[
-            pltpu.VMEM((tiles * LANES, LANES), jnp.float32),
+            pltpu.VMEM((tiles * FEATURES, LANES), jnp.float32),
             pltpu.VMEM(block_list.shape, jnp.int32),
             pltpu.SMEM(tile_counts.shape, jnp.int32),
             pltpu.VMEM(positions.shape, jnp.float32),

time: 38.1 us -> 36.8 us (0.966)
  the two profiles are of different devices: /device:TPU:15 before, /device:TPU:3 now
where the time goes in v3:
time: 36.8 us; the launch traced here: 36.6 us
  Pallas kernels  21 us (57%)
  starting transfers between devices  9.21 us (25%)
  waiting for transfers between devices  6.21 us (17%)
    pallas_call x1, Pallas kernels, shards(): pl.pallas_call(far_kernel, out_shape=jax.ShapeDtypeStruct((3, count), jnp...  13.1 us
    ppermute x8, starting transfers between devices, swap(): return lax.ppermute(value, axis, [(i, i ^ bits) for i in range(size)])  9.21 us
    ppermute x8, waiting for transfers between devices, swap(): return lax.ppermute(value, axis, [(i, i ^ bits) for i in range(size)])  6.21 us
    pallas_call x1, Pallas kernels, shards(): total = near_pairs(near_list, origin, left, near, near_twin)  5.47 us
    pallas_call x1, Pallas kernels, shards(): tiled, origin, left, near_list, far_list, own = prepare(here, *held)  2.35 us
  transfers between devices with their start and end apart: 8, of which 3 were waited for; matrix products, arithmetic and copies ran while one was open for 0% of the time, Pallas kernels for 6%

profile of v3, /device:TPU:3, one launch (start us, length us, event | category | flops | bytes accessed | tf_op | source)
XLA Modules:
  0.0 36.6 jit_solution(8021857622332110249)
XLA Ops:
  0.0 0.0 collective-permute-start
  0.0 2.4 %collective-permute-start.2 = (f32[10,512]{1,0:T(8,128)}, f32[10,512]{1,0:T(8,128)S(1)}, u32[]{:S(2)}, u32[]{:S(2)}) collective-permute-start(f32[10,512]{1,0:T(8,128)} %nodes_hbm.1), channel_id=1, source_target_pairs={{0,24},{8,16},{16,8},{24,0},{1,25},{9,17},{17,9},{25,1},{2,26},{10... | collective-permute-start | bytes 61448 | tf_op jit(solution)/shard_map/ppermute | solution.py:429
  2.4 0.2 collective-permute-start.1
  2.7 0.1 pad_add_fusion.self_ref
  2.7 2.4 %shard_map.55 = (f32[3,16,128]{2,1,0:T(8,128)S(1)}, f32[3,128]{1,0:T(4,128)S(1)}, bf16[16,128,128]{2,1,0:T(8,128)(2,1)S(1)}, s32[1,384]{1,0:T(1,128)S(1)}, s32[1,384]{1,0:T(1,128)S(1)}, /*index=5*/f32[40,128]{1,0:T(8,128)S(1)}) custom-call(s32[2]{0:T(128)S(1)} %pad_add_fusion.self_ref, s32[16,16]{1,0:T(8,128)} %lists_hbm.1, s32[16]{0:T(128)} %counts_hbm.1, ...), custom_call_target="tpu_custom_call" | custom-call | flops 10000000000 | bytes 1000000 | tf_op jit(solution)/shard_map/pallas_call | solution.py:471
  5.1 0.0 collective-permute-done
  5.1 0.0 collective-permute-done.2
  5.1 0.6 %collective-permute-done.1 = f32[10,512]{1,0:T(8,128)S(1)} collective-permute-done((f32[10,512]{1,0:T(8,128)}, f32[10,512]{1,0:T(8,128)S(1)}, u32[]{:S(2)}, u32[]{:S(2)}) %collective-permute-start.1) | collective-permute-done | bytes 20512 | tf_op jit(solution)/shard_map/ppermute | solution.py:429
  5.8 3.5 %collective-permute-start.5 = (f32[4,40,128]{2,1,0:T(8,128)S(1)}, f32[4,40,128]{2,1,0:T(8,128)S(1)}, u32[]{:S(2)}, u32[]{:S(2)}) collective-permute-start(f32[4,40,128]{2,1,0:T(8,128)S(1)} %pad_maximum_fusion.1.mine_ref), channel_id=1, source_target_pairs={{0,6},{1,7},{2,4},{3,5},{4,2},{5,3},{6,0},{7,1},{8,14},{9,15},{10,... | collective-permute-start | bytes 245768 | tf_op jit(solution)/shard_map/ppermute | solution.py:429
  9.2 0.0 collective-permute-start.4
  9.2 0.4 collective-permute-start.3
  9.6 2.6 %collective-permute-start.6 = (f32[4,40,128]{2,1,0:T(8,128)S(1)}, f32[4,40,128]{2,1,0:T(8,128)S(1)}, u32[]{:S(2)}, u32[]{:S(2)}) collective-permute-start(f32[4,40,128]{2,1,0:T(8,128)S(1)} %pad_maximum_fusion.1.mine_ref), channel_id=1, source_target_pairs={{0,1},{1,0},{2,3},{3,2},{4,5},{5,4},{6,7},{7,6},{8,9},{9,8},{10,11... | collective-permute-start | bytes 245768 | tf_op jit(solution)/shard_map/ppermute | solution.py:429
  12.3 0.0 collective-permute-done.5
  12.3 4.1 %collective-permute-done.4 = f32[4,40,128]{2,1,0:T(8,128)S(1)} collective-permute-done((f32[4,40,128]{2,1,0:T(8,128)S(1)}, f32[4,40,128]{2,1,0:T(8,128)S(1)}, u32[]{:S(2)}, u32[]{:S(2)}) %collective-permute-start.4) | collective-permute-done | bytes 81952 | tf_op jit(solution)/shard_map/ppermute | solution.py:429
  16.3 0.0 collective-permute-done.3
  16.4 0.0 collective-permute-done.6.twin_ref
  16.4 0.0 copy-start
  16.4 5.5 %shard_map.56.start_ref = f32[17,128,128]{2,1,0:T(8,128)S(1)} custom-call(s32[1,384]{1,0:T(1,128)S(1)} %get-tuple-element.22.list_ref, f32[3,128]{1,0:T(4,128)S(1)} %get-tuple-element.19.origin_ref, bf16[16,128,128]{2,1,0:T(8,128)(2,1)S(1)} %get-tuple-element.20.left_ref, f32[4,40,128]{2,1,0:T(8,128)S(1)} %pad_maximum_fusion.1.mine_ref, ...), custom_call_target="tpu_custom_call" | custom-call | flops 10000000000 | bytes 1000000 | tf_op jit(solution)/shard_map/pallas_call | solution.py:487
  21.9 0.1 collective-permute-start.7
  21.9 1.5 %collective-permute-done.7.twin_ref = f32[12,40,128]{2,1,0:T(8,128)S(1)} collective-permute-done((f32[12,40,128]{2,1,0:T(8,128)S(1)}, f32[12,40,128]{2,1,0:T(8,128)S(1)}, u32[]{:S(2)}, u32[]{:S(2)}) %collective-permute-start.7) | collective-permute-done | bytes 245792 | tf_op jit(solution)/shard_map/ppermute | solution.py:429
  23.4 0.0 copy-done
  23.5 13.1 %shard_map.57 = f32[3,2048]{1,0:T(4,128)} custom-call(s32[1,384]{1,0:T(1,128)S(1)} %get-tuple-element.15.list_ref, f32[3,16,128]{2,1,0:T(8,128)S(1)} %get-tuple-element.16.tiled_ref, f32[3,128]{1,0:T(4,128)S(1)} %get-tuple-element.19.origin_ref, bf16[16,128,128]{2,1,0:T(8,128)(2,1)S(1)} %get-tuple-element.20.left_ref, s32[1,2048]{1,0:T(1,128)S(1)} %copy-done, ...), custom_call_target="tpu_custom_call" | custom-call | tf_op jit(solution)/shard_map/pallas_call | solution.py:492
  (5 shorter events, 0.0 us)
Async XLA Ops:
  0.0 5.1 %collective-permute-start = (f32[10,512]{1,0:T(8,128)}, f32[10,512]{1,0:T(8,128)S(1)}, u32[]{:S(2)}, u32[]{:S(2)}) collective-permute-start(f32[10,512]{1,0:T(8,128)} %nodes_hbm.1), channel_id=1, source_target_pairs={{0,8},{8,0},{16,24},{24,16},{1,9},{9,1},{17,25},{25,17},{2,10},{10... | collective-permute-start | bytes 61448 | tf_op jit(solution)/shard_map/ppermute | solution.py:429
  0.0 5.1 %collective-permute-start.2 = (f32[10,512]{1,0:T(8,128)}, f32[10,512]{1,0:T(8,128)S(1)}, u32[]{:S(2)}, u32[]{:S(2)}) collective-permute-start(f32[10,512]{1,0:T(8,128)} %nodes_hbm.1), channel_id=1, source_target_pairs={{0,24},{8,16},{16,8},{24,0},{1,25},{9,17},{17,9},{25,1},{2,26},{10... | collective-permute-start | bytes 61448 | tf_op jit(solution)/shard_map/ppermute | solution.py:429
  2.4 3.3 %collective-permute-start.1 = (f32[10,512]{1,0:T(8,128)}, f32[10,512]{1,0:T(8,128)S(1)}, u32[]{:S(2)}, u32[]{:S(2)}) collective-permute-start(f32[10,512]{1,0:T(8,128)} %nodes_hbm.1), channel_id=1, source_target_pairs={{0,16},{8,24},{16,0},{24,8},{1,17},{9,25},{17,1},{25,9},{2,18},{10... | collective-permute-start | bytes 61448 | tf_op jit(solution)/shard_map/ppermute | solution.py:429
  5.8 6.5 %collective-permute-start.5 = (f32[4,40,128]{2,1,0:T(8,128)S(1)}, f32[4,40,128]{2,1,0:T(8,128)S(1)}, u32[]{:S(2)}, u32[]{:S(2)}) collective-permute-start(f32[4,40,128]{2,1,0:T(8,128)S(1)} %pad_maximum_fusion.1.mine_ref), channel_id=1, source_target_pairs={{0,6},{1,7},{2,4},{3,5},{4,2},{5,3},{6,0},{7,1},{8,14},{9,15},{10,... | collective-permute-start | bytes 245768 | tf_op jit(solution)/shard_map/ppermute | solution.py:429
  9.2 7.1 %collective-permute-start.4 = (f32[4,40,128]{2,1,0:T(8,128)S(1)}, f32[4,40,128]{2,1,0:T(8,128)S(1)}, u32[]{:S(2)}, u32[]{:S(2)}) collective-permute-start(f32[4,40,128]{2,1,0:T(8,128)S(1)} %pad_maximum_fusion.1.mine_ref), channel_id=1, source_target_pairs={{0,4},{1,5},{2,6},{3,7},{4,0},{5,1},{6,2},{7,3},{8,12},{9,13},{10,... | collective-permute-start | bytes 245768 | tf_op jit(solution)/shard_map/ppermute | solution.py:429
  9.2 7.1 %collective-permute-start.3 = (f32[4,40,128]{2,1,0:T(8,128)S(1)}, f32[4,40,128]{2,1,0:T(8,128)S(1)}, u32[]{:S(2)}, u32[]{:S(2)}) collective-permute-start(f32[4,40,128]{2,1,0:T(8,128)S(1)} %pad_maximum_fusion.1.mine_ref), channel_id=1, source_target_pairs={{0,2},{1,3},{2,0},{3,1},{4,6},{5,7},{6,4},{7,5},{8,10},{9,11},{10,... | collective-permute-start | bytes 245768 | tf_op jit(solution)/shard_map/ppermute | solution.py:429
  9.6 6.8 %collective-permute-start.6 = (f32[4,40,128]{2,1,0:T(8,128)S(1)}, f32[4,40,128]{2,1,0:T(8,128)S(1)}, u32[]{:S(2)}, u32[]{:S(2)}) collective-permute-start(f32[4,40,128]{2,1,0:T(8,128)S(1)} %pad_maximum_fusion.1.mine_ref), channel_id=1, source_target_pairs={{0,1},{1,0},{2,3},{3,2},{4,5},{5,4},{6,7},{7,6},{8,9},{9,8},{10,11... | collective-permute-start | bytes 245768 | tf_op jit(solution)/shard_map/ppermute | solution.py:429
  16.4 7.1 %copy-start = (s32[1,2048]{1,0:T(1,128)S(1)}, s32[1,2048]{1,0:T(1,128)}, u32[]{:S(2)}) copy-start(s32[1,2048]{1,0:T(1,128)} %slot_ref.1) | copy-start | bytes 24580
  21.9 1.6 %collective-permute-start.7 = (f32[12,40,128]{2,1,0:T(8,128)S(1)}, f32[12,40,128]{2,1,0:T(8,128)S(1)}, u32[]{:S(2)}, u32[]{:S(2)}) collective-permute-start(f32[12,40,128]{2,1,0:T(8,128)S(1)} %pad_maximum_fusion.mine_ref), channel_id=1, source_target_pairs={{0,1},{1,0},{2,3},{3,2},{4,5},{5,4},{6,7},{7,6},{8,9},{9,8},{10,11... | collective-permute-start | bytes 737288 | tf_op jit(solution)/shard_map/ppermute | solution.py:429

commit v4 on v3

--- a/solution.py
+++ b/solution.py
@@ -12,6 +12,7 @@
 LANES = 128
 SUBS = 8
 PAIRS = 8
+LAG = 2
 FEATURES = 48
 WEIGHTS = 40
 BLOCK_ROOM = 2**16
@@ -338,23 +339,26 @@
         add_forces(terms_ref.at[u], take, total_ref, pair[0])
 
     def step(i, carry):
-        pairs, last = carry
+        pairs, lasts = carry
         nexts = []
-        behind(PAIRS - 1, last)
+        for u in range(LAG):
+            behind(PAIRS - LAG + u, lasts[u])
         for u in range(PAIRS):
             pair_terms(near_ref.at[u], terms_ref.at[u])
             nexts.append(ahead(u, (i + 1) * PAIRS + u))
-            if u + 1 < PAIRS:
+            if u + LAG < PAIRS:
                 behind(u, pairs[u])
-        return tuple(nexts), pairs[-1]
+        return tuple(nexts), pairs[-LAG:]
 
     pairs = tuple(ahead(u, u) for u in range(PAIRS))
     none = (jnp.int32(tiles), jnp.int32(0))
-    terms_ref[PAIRS - 1] = jnp.zeros(terms_ref.shape[1:], terms_ref.dtype)
+    for u in range(PAIRS - LAG, PAIRS):
+        terms_ref[u] = jnp.zeros(terms_ref.shape[1:], terms_ref.dtype)
     live = list_ref[0, list_ref.shape[1] - 1]
     steps = quotient(live + (PAIRS - 1), PAIRS)
-    carry = lax.fori_loop(0, steps, step, (pairs, none))
-    behind(PAIRS - 1, carry[-1])
+    carry = lax.fori_loop(0, steps, step, (pairs, (none,) * LAG))
+    for u in range(LAG):
+        behind(PAIRS - LAG + u, carry[-1][u])
 
 
 def near_kernel(list_ref, origin_ref, left_ref, mine_ref, twin_ref, total_ref, *scratch):

time: 36.8 us -> 36.3 us (0.986)
  Pallas kernels: 21 us -> 20.5 us
  transfers between devices with their start and end apart: 8 -> 8, of which waited for: 3 -> 3; matrix products, arithmetic and copies ran while one was open for 0% -> 0% of each run, Pallas kernels for 6% -> 7%
where the time goes in v4:
time: 36.3 us; the launch traced here: 36.2 us
  Pallas kernels  20.5 us (56%)
  starting transfers between devices  9.21 us (25%)
  waiting for transfers between devices  6.21 us (17%)
    pallas_call x1, Pallas kernels, shards(): pl.pallas_call(far_kernel, out_shape=jax.ShapeDtypeStruct((3, count), jnp...  12.8 us
    ppermute x8, starting transfers between devices, swap(): return lax.ppermute(value, axis, [(i, i ^ bits) for i in range(size)])  9.21 us
    ppermute x8, waiting for transfers between devices, swap(): return lax.ppermute(value, axis, [(i, i ^ bits) for i in range(size)])  6.21 us
    pallas_call x1, Pallas kernels, shards(): total = near_pairs(near_list, origin, left, near, near_twin)  5.41 us
    pallas_call x1, Pallas kernels, shards(): tiled, origin, left, near_list, far_list, own = prepare(here, *held)  2.35 us
  transfers between devices with their start and end apart: 8, of which 3 were waited for; matrix products, arithmetic and copies ran while one was open for 0% of the time, Pallas kernels for 7%

profile of v4, /device:TPU:3, one launch (start us, length us, event | category | flops | bytes accessed | tf_op | source)
XLA Modules:
  0.0 36.2 jit_solution(9703725896042434115)
XLA Ops:
  0.0 0.0 collective-permute-start
  0.0 2.4 %collective-permute-start.2 = (f32[10,512]{1,0:T(8,128)}, f32[10,512]{1,0:T(8,128)S(1)}, u32[]{:S(2)}, u32[]{:S(2)}) collective-permute-start(f32[10,512]{1,0:T(8,128)} %nodes_hbm.1), channel_id=1, source_target_pairs={{0,24},{8,16},{16,8},{24,0},{1,25},{9,17},{17,9},{25,1},{2,26},{10... | collective-permute-start | bytes 61448 | tf_op jit(solution)/shard_map/ppermute | solution.py:433
  2.4 0.2 collective-permute-start.1
  2.7 0.1 pad_add_fusion.self_ref
  2.7 2.4 %shard_map.55 = (f32[3,16,128]{2,1,0:T(8,128)S(1)}, f32[3,128]{1,0:T(4,128)S(1)}, bf16[16,128,128]{2,1,0:T(8,128)(2,1)S(1)}, s32[1,384]{1,0:T(1,128)S(1)}, s32[1,384]{1,0:T(1,128)S(1)}, /*index=5*/f32[40,128]{1,0:T(8,128)S(1)}) custom-call(s32[2]{0:T(128)S(1)} %pad_add_fusion.self_ref, s32[16,16]{1,0:T(8,128)} %lists_hbm.1, s32[16]{0:T(128)} %counts_hbm.1, ...), custom_call_target="tpu_custom_call" | custom-call | flops 10000000000 | bytes 1000000 | tf_op jit(solution)/shard_map/pallas_call | solution.py:475
  5.1 0.0 collective-permute-done
  5.1 0.0 collective-permute-done.2
  5.1 0.6 %collective-permute-done.1 = f32[10,512]{1,0:T(8,128)S(1)} collective-permute-done((f32[10,512]{1,0:T(8,128)}, f32[10,512]{1,0:T(8,128)S(1)}, u32[]{:S(2)}, u32[]{:S(2)}) %collective-permute-start.1) | collective-permute-done | bytes 20512 | tf_op jit(solution)/shard_map/ppermute | solution.py:433
  5.8 3.5 %collective-permute-start.5 = (f32[4,40,128]{2,1,0:T(8,128)S(1)}, f32[4,40,128]{2,1,0:T(8,128)S(1)}, u32[]{:S(2)}, u32[]{:S(2)}) collective-permute-start(f32[4,40,128]{2,1,0:T(8,128)S(1)} %pad_maximum_fusion.1.mine_ref), channel_id=1, source_target_pairs={{0,6},{1,7},{2,4},{3,5},{4,2},{5,3},{6,0},{7,1},{8,14},{9,15},{10,... | collective-permute-start | bytes 245768 | tf_op jit(solution)/shard_map/ppermute | solution.py:433
  9.2 0.0 collective-permute-start.4
  9.2 0.4 collective-permute-start.3
  9.6 2.6 %collective-permute-start.6 = (f32[4,40,128]{2,1,0:T(8,128)S(1)}, f32[4,40,128]{2,1,0:T(8,128)S(1)}, u32[]{:S(2)}, u32[]{:S(2)}) collective-permute-start(f32[4,40,128]{2,1,0:T(8,128)S(1)} %pad_maximum_fusion.1.mine_ref), channel_id=1, source_target_pairs={{0,1},{1,0},{2,3},{3,2},{4,5},{5,4},{6,7},{7,6},{8,9},{9,8},{10,11... | collective-permute-start | bytes 245768 | tf_op jit(solution)/shard_map/ppermute | solution.py:433
  12.3 0.0 collective-permute-done.5
  12.3 4.1 %collective-permute-done.4 = f32[4,40,128]{2,1,0:T(8,128)S(1)} collective-permute-done((f32[4,40,128]{2,1,0:T(8,128)S(1)}, f32[4,40,128]{2,1,0:T(8,128)S(1)}, u32[]{:S(2)}, u32[]{:S(2)}) %collective-permute-start.4) | collective-permute-done | bytes 81952 | tf_op jit(solution)/shard_map/ppermute | solution.py:433
  16.3 0.0 collective-permute-done.3
  16.4 0.0 collective-permute-done.6.twin_ref
  16.4 0.0 copy-start
  16.4 5.4 %shard_map.56.start_ref = f32[17,128,128]{2,1,0:T(8,128)S(1)} custom-call(s32[1,384]{1,0:T(1,128)S(1)} %get-tuple-element.22.list_ref, f32[3,128]{1,0:T(4,128)S(1)} %get-tuple-element.19.origin_ref, bf16[16,128,128]{2,1,0:T(8,128)(2,1)S(1)} %get-tuple-element.20.left_ref, f32[4,40,128]{2,1,0:T(8,128)S(1)} %pad_maximum_fusion.1.mine_ref, ...), custom_call_target="tpu_custom_call" | custom-call | flops 10000000000 | bytes 1000000 | tf_op jit(solution)/shard_map/pallas_call | solution.py:491
  21.8 0.1 collective-permute-start.7
  21.9 1.5 %collective-permute-done.7.twin_ref = f32[12,40,128]{2,1,0:T(8,128)S(1)} collective-permute-done((f32[12,40,128]{2,1,0:T(8,128)S(1)}, f32[12,40,128]{2,1,0:T(8,128)S(1)}, u32[]{:S(2)}, u32[]{:S(2)}) %collective-permute-start.7) | collective-permute-done | bytes 245792 | tf_op jit(solution)/shard_map/ppermute | solution.py:433
  23.4 0.0 copy-done
  23.4 12.8 %shard_map.57 = f32[3,2048]{1,0:T(4,128)} custom-call(s32[1,384]{1,0:T(1,128)S(1)} %get-tuple-element.15.list_ref, f32[3,16,128]{2,1,0:T(8,128)S(1)} %get-tuple-element.16.tiled_ref, f32[3,128]{1,0:T(4,128)S(1)} %get-tuple-element.19.origin_ref, bf16[16,128,128]{2,1,0:T(8,128)(2,1)S(1)} %get-tuple-element.20.left_ref, s32[1,2048]{1,0:T(1,128)S(1)} %copy-done, ...), custom_call_target="tpu_custom_call" | custom-call | tf_op jit(solution)/shard_map/pallas_call | solution.py:496
  (5 shorter events, 0.0 us)
Async XLA Ops:
  0.0 5.1 %collective-permute-start = (f32[10,512]{1,0:T(8,128)}, f32[10,512]{1,0:T(8,128)S(1)}, u32[]{:S(2)}, u32[]{:S(2)}) collective-permute-start(f32[10,512]{1,0:T(8,128)} %nodes_hbm.1), channel_id=1, source_target_pairs={{0,8},{8,0},{16,24},{24,16},{1,9},{9,1},{17,25},{25,17},{2,10},{10... | collective-permute-start | bytes 61448 | tf_op jit(solution)/shard_map/ppermute | solution.py:433
  0.0 5.1 %collective-permute-start.2 = (f32[10,512]{1,0:T(8,128)}, f32[10,512]{1,0:T(8,128)S(1)}, u32[]{:S(2)}, u32[]{:S(2)}) collective-permute-start(f32[10,512]{1,0:T(8,128)} %nodes_hbm.1), channel_id=1, source_target_pairs={{0,24},{8,16},{16,8},{24,0},{1,25},{9,17},{17,9},{25,1},{2,26},{10... | collective-permute-start | bytes 61448 | tf_op jit(solution)/shard_map/ppermute | solution.py:433
  2.4 3.3 %collective-permute-start.1 = (f32[10,512]{1,0:T(8,128)}, f32[10,512]{1,0:T(8,128)S(1)}, u32[]{:S(2)}, u32[]{:S(2)}) collective-permute-start(f32[10,512]{1,0:T(8,128)} %nodes_hbm.1), channel_id=1, source_target_pairs={{0,16},{8,24},{16,0},{24,8},{1,17},{9,25},{17,1},{25,9},{2,18},{10... | collective-permute-start | bytes 61448 | tf_op jit(solution)/shard_map/ppermute | solution.py:433
  5.8 6.5 %collective-permute-start.5 = (f32[4,40,128]{2,1,0:T(8,128)S(1)}, f32[4,40,128]{2,1,0:T(8,128)S(1)}, u32[]{:S(2)}, u32[]{:S(2)}) collective-permute-start(f32[4,40,128]{2,1,0:T(8,128)S(1)} %pad_maximum_fusion.1.mine_ref), channel_id=1, source_target_pairs={{0,6},{1,7},{2,4},{3,5},{4,2},{5,3},{6,0},{7,1},{8,14},{9,15},{10,... | collective-permute-start | bytes 245768 | tf_op jit(solution)/shard_map/ppermute | solution.py:433
  9.2 7.1 %collective-permute-start.4 = (f32[4,40,128]{2,1,0:T(8,128)S(1)}, f32[4,40,128]{2,1,0:T(8,128)S(1)}, u32[]{:S(2)}, u32[]{:S(2)}) collective-permute-start(f32[4,40,128]{2,1,0:T(8,128)S(1)} %pad_maximum_fusion.1.mine_ref), channel_id=1, source_target_pairs={{0,4},{1,5},{2,6},{3,7},{4,0},{5,1},{6,2},{7,3},{8,12},{9,13},{10,... | collective-permute-start | bytes 245768 | tf_op jit(solution)/shard_map/ppermute | solution.py:433
  9.2 7.1 %collective-permute-start.3 = (f32[4,40,128]{2,1,0:T(8,128)S(1)}, f32[4,40,128]{2,1,0:T(8,128)S(1)}, u32[]{:S(2)}, u32[]{:S(2)}) collective-permute-start(f32[4,40,128]{2,1,0:T(8,128)S(1)} %pad_maximum_fusion.1.mine_ref), channel_id=1, source_target_pairs={{0,2},{1,3},{2,0},{3,1},{4,6},{5,7},{6,4},{7,5},{8,10},{9,11},{10,... | collective-permute-start | bytes 245768 | tf_op jit(solution)/shard_map/ppermute | solution.py:433
  9.6 6.8 %collective-permute-start.6 = (f32[4,40,128]{2,1,0:T(8,128)S(1)}, f32[4,40,128]{2,1,0:T(8,128)S(1)}, u32[]{:S(2)}, u32[]{:S(2)}) collective-permute-start(f32[4,40,128]{2,1,0:T(8,128)S(1)} %pad_maximum_fusion.1.mine_ref), channel_id=1, source_target_pairs={{0,1},{1,0},{2,3},{3,2},{4,5},{5,4},{6,7},{7,6},{8,9},{9,8},{10,11... | collective-permute-start | bytes 245768 | tf_op jit(solution)/shard_map/ppermute | solution.py:433
  16.4 7.0 %copy-start = (s32[1,2048]{1,0:T(1,128)S(1)}, s32[1,2048]{1,0:T(1,128)}, u32[]{:S(2)}) copy-start(s32[1,2048]{1,0:T(1,128)} %slot_ref.1) | copy-start | bytes 24580
  21.8 1.6 %collective-permute-start.7 = (f32[12,40,128]{2,1,0:T(8,128)S(1)}, f32[12,40,128]{2,1,0:T(8,128)S(1)}, u32[]{:S(2)}, u32[]{:S(2)}) collective-permute-start(f32[12,40,128]{2,1,0:T(8,128)S(1)} %pad_maximum_fusion.mine_ref), channel_id=1, source_target_pairs={{0,1},{1,0},{2,3},{3,2},{4,5},{5,4},{6,7},{7,6},{8,9},{9,8},{10,11... | collective-permute-start | bytes 737288 | tf_op jit(solution)/shard_map/ppermute | solution.py:433

commit v5 on v4

--- a/solution.py
+++ b/solution.py
@@ -11,7 +11,7 @@
 
 LANES = 128
 SUBS = 8
-PAIRS = 8
+PAIRS = 6
 LAG = 2
 FEATURES = 48
 WEIGHTS = 40
@@ -81,6 +81,7 @@
     near_list_ref,
     far_list_ref,
     own_ref,
+    hot_ref,
     rows_ref,
     lists_ref,
     counts_ref,
@@ -111,6 +112,7 @@
     slots = slot_ref[...]
     owner = owners(slots, tiles, count)
     hot = hot_lanes(slots, count)
+    hot_ref[...] = hot
     rows = []
     for c in range(3):
         value = pos_ref[c : c + 1, :]
@@ -372,6 +374,7 @@
     origin_ref,
     left_ref,
     slot_ref,
+    hot_ref,
     mine_ref,
     twin_ref,
     start_ref,
@@ -408,7 +411,7 @@
     parts = [part.astype(jnp.bfloat16) for force in forces for part in thirds(force)]
     got = jnp.dot(
         jnp.concatenate(parts, axis=0),
-        hot_lanes(slots, count),
+        hot_ref[...],
         preferred_element_type=jnp.float32,
     )
     for c in range(3):
@@ -453,9 +456,10 @@
             jax.ShapeDtypeStruct((1, room), jnp.int32),
             jax.ShapeDtypeStruct((1, room), jnp.int32),
             jax.ShapeDtypeStruct((10 * each, LANES), jnp.float32),
+            jax.ShapeDtypeStruct((LANES, count), jnp.bfloat16),
         ),
         in_specs=[smem] + [pl.BlockSpec(memory_space=pltpu.HBM)] * 5,
-        out_specs=(vmem,) * 6,
+        out_specs=(vmem,) * 7,
         scratch_shapes=[
             pltpu.VMEM((tiles * FEATURES, LANES), jnp.float32),
             pltpu.VMEM(block_list.shape, jnp.int32),
@@ -472,7 +476,7 @@
         pltpu.with_memory_space_constraint(value, pltpu.HBM)
         for value in (block_list, tile_counts, positions, slot_of, node_moments)
     ]
-    tiled, origin, left, near_list, far_list, own = prepare(here, *held)
+    tiled, origin, left, near_list, far_list, own, hot = prepare(here, *held)
     near = [swap(node_moments, "gx", gx, b) for b in range(1, gx)]
     near = jnp.stack([own] + [value.reshape(10 * each, LANES) for value in near])
     near, origin = lax.optimization_barrier((near, origin))
@@ -496,7 +500,7 @@
     return pl.pallas_call(
         far_kernel,
         out_shape=jax.ShapeDtypeStruct((3, count), jnp.float32),
-        in_specs=[smem] + [vmem] * 7,
+        in_specs=[smem] + [vmem] * 8,
         out_specs=vmem,
         scratch_shapes=[
             pltpu.VMEM((tiles + 1, LANES, LANES), jnp.float32),
@@ -504,7 +508,7 @@
         ]
         + far_work,
         compiler_params=far_params,
-    )(far_list, tiled, origin, left, slot_of, far, far_twin, total)
+    )(far_list, tiled, origin, left, slot_of, hot, far, far_twin, total)
 
 
 def solution(mesh):

time: 36.3 us -> 36.7 us (1.011)
  Pallas kernels: 20.5 us -> 20.9 us
  transfers between devices with their start and end apart: 8 -> 8, of which waited for: 3 -> 3; matrix products, arithmetic and copies ran while one was open for 0% -> 0% of each run, Pallas kernels for 7% -> 6%
where the time goes in v5:
time: 36.7 us; the launch traced here: 36.5 us
  Pallas kernels  20.9 us (57%)
  starting transfers between devices  9.21 us (25%)
  waiting for transfers between devices  6.21 us (17%)
    pallas_call x1, Pallas kernels, shards(): pl.pallas_call(far_kernel, out_shape=jax.ShapeDtypeStruct((3, count), jnp...  12.9 us
    ppermute x8, starting transfers between devices, swap(): return lax.ppermute(value, axis, [(i, i ^ bits) for i in range(size)])  9.21 us
    ppermute x8, waiting for transfers between devices, swap(): return lax.ppermute(value, axis, [(i, i ^ bits) for i in range(size)])  6.21 us
    pallas_call x1, Pallas kernels, shards(): total = near_pairs(near_list, origin, left, near, near_twin)  5.65 us
    pallas_call x1, Pallas kernels, shards(): tiled, origin, left, near_list, far_list, own, hot = prepare(here, *held)  2.36 us
  transfers between devices with their start and end apart: 8, of which 3 were waited for; matrix products, arithmetic and copies ran while one was open for 0% of the time, Pallas kernels for 6%

profile of v5, /device:TPU:3, one launch (start us, length us, event | category | flops | bytes accessed | tf_op | source)
XLA Modules:
  0.0 36.5 jit_solution(11267522566612274629)
XLA Ops:
  0.0 0.0 collective-permute-start
  0.0 2.4 %collective-permute-start.2 = (f32[10,512]{1,0:T(8,128)}, f32[10,512]{1,0:T(8,128)S(1)}, u32[]{:S(2)}, u32[]{:S(2)}) collective-permute-start(f32[10,512]{1,0:T(8,128)} %nodes_hbm.1), channel_id=1, source_target_pairs={{0,24},{8,16},{16,8},{24,0},{1,25},{9,17},{17,9},{25,1},{2,26},{10... | collective-permute-start | bytes 61448 | tf_op jit(solution)/shard_map/ppermute | solution.py:436
  2.4 0.2 collective-permute-start.1
  2.7 0.1 pad_add_fusion.self_ref
  2.7 2.4 %shard_map.55 = (f32[3,16,128]{2,1,0:T(8,128)S(1)}, f32[3,128]{1,0:T(4,128)S(1)}, bf16[16,128,128]{2,1,0:T(8,128)(2,1)S(1)}, s32[1,384]{1,0:T(1,128)S(1)}, s32[1...) custom-call(s32[2]{0:T(128)S(1)} %pad_add_fusion.self_ref, s32[16,16]{1,0:T(8,128)} %lists_hbm.1, ...), custom_call_target="tpu_custom_call" | custom-call | flops 10000000000 | bytes 1000000 | tf_op jit(solution)/shard_map/pallas_call | solution.py:479
  5.1 0.0 collective-permute-done
  5.1 0.0 collective-permute-done.2
  5.1 0.6 %collective-permute-done.1 = f32[10,512]{1,0:T(8,128)S(1)} collective-permute-done((f32[10,512]{1,0:T(8,128)}, f32[10,512]{1,0:T(8,128)S(1)}, u32[]{:S(2)}, u32[]{:S(2)}) %collective-permute-start.1) | collective-permute-done | bytes 20512 | tf_op jit(solution)/shard_map/ppermute | solution.py:436
  5.8 3.5 %collective-permute-start.5 = (f32[4,40,128]{2,1,0:T(8,128)S(1)}, f32[4,40,128]{2,1,0:T(8,128)S(1)}, u32[]{:S(2)}, u32[]{:S(2)}) collective-permute-start(f32[4,40,128]{2,1,0:T(8,128)S(1)} %pad_maximum_fusion.1.mine_ref), channel_id=1, source_target_pairs={{0,6},{1,7},{2,4},{3,5},{4,2},{5,3},{6,0},{7,1},{8,14},{9,15},{10,... | collective-permute-start | bytes 245768 | tf_op jit(solution)/shard_map/ppermute | solution.py:436
  9.2 0.0 collective-permute-start.4
  9.2 0.4 collective-permute-start.3
  9.6 2.6 %collective-permute-start.6 = (f32[4,40,128]{2,1,0:T(8,128)S(1)}, f32[4,40,128]{2,1,0:T(8,128)S(1)}, u32[]{:S(2)}, u32[]{:S(2)}) collective-permute-start(f32[4,40,128]{2,1,0:T(8,128)S(1)} %pad_maximum_fusion.1.mine_ref), channel_id=1, source_target_pairs={{0,1},{1,0},{2,3},{3,2},{4,5},{5,4},{6,7},{7,6},{8,9},{9,8},{10,11... | collective-permute-start | bytes 245768 | tf_op jit(solution)/shard_map/ppermute | solution.py:436
  12.3 0.0 collective-permute-done.5
  12.3 4.1 %collective-permute-done.4 = f32[4,40,128]{2,1,0:T(8,128)S(1)} collective-permute-done((f32[4,40,128]{2,1,0:T(8,128)S(1)}, f32[4,40,128]{2,1,0:T(8,128)S(1)}, u32[]{:S(2)}, u32[]{:S(2)}) %collective-permute-start.4) | collective-permute-done | bytes 81952 | tf_op jit(solution)/shard_map/ppermute | solution.py:436
  16.3 0.0 collective-permute-done.3
  16.4 0.0 collective-permute-done.6.twin_ref
  16.4 0.0 copy-start
  16.4 5.7 %shard_map.56.start_ref = f32[17,128,128]{2,1,0:T(8,128)S(1)} custom-call(s32[1,384]{1,0:T(1,128)S(1)} %get-tuple-element.24.list_ref, f32[3,128]{1,0:T(4,128)S(1)} %get-tuple-element.20.origin_ref, bf16[16,128,128]{2,1,0:T(8,128)(2,1)S(1)} %get-tuple-element.21.left_ref, f32[4,40,128]{2,1,0:T(8,128)S(1)} %pad_maximum_fusion.1.mine_ref, ...), custom_call_target="tpu_custom_call" | custom-call | flops 10000000000 | bytes 1000000 | tf_op jit(solution)/shard_map/pallas_call | solution.py:495
  22.1 0.1 collective-permute-start.7
  22.1 1.5 %collective-permute-done.7.twin_ref = f32[12,40,128]{2,1,0:T(8,128)S(1)} collective-permute-done((f32[12,40,128]{2,1,0:T(8,128)S(1)}, f32[12,40,128]{2,1,0:T(8,128)S(1)}, u32[]{:S(2)}, u32[]{:S(2)}) %collective-permute-start.7) | collective-permute-done | bytes 245792 | tf_op jit(solution)/shard_map/ppermute | solution.py:436
  23.6 0.0 copy-done
  23.6 12.9 %shard_map.57 = f32[3,2048]{1,0:T(4,128)} custom-call(s32[1,384]{1,0:T(1,128)S(1)} %get-tuple-element.16.list_ref, f32[3,16,128]{2,1,0:T(8,128)S(1)} %get-tuple-element.17.tiled_ref, f32[3,128]{1,0:T(4,128)S(1)} %get-tuple-element.20.origin_ref, bf16[16,128,128]{2,1,0:T(8,128)(2,1)S(1)} %get-tuple-element.21.left_ref, s32[1,2048]{1,0:T(1,128)S(1)} %copy-done, ...), custom_call_target="tpu_custom_call" | custom-call | tf_op jit(solution)/shard_map/pallas_call | solution.py:500
  (5 shorter events, 0.0 us)
Async XLA Ops:
  0.0 5.1 %collective-permute-start = (f32[10,512]{1,0:T(8,128)}, f32[10,512]{1,0:T(8,128)S(1)}, u32[]{:S(2)}, u32[]{:S(2)}) collective-permute-start(f32[10,512]{1,0:T(8,128)} %nodes_hbm.1), channel_id=1, source_target_pairs={{0,8},{8,0},{16,24},{24,16},{1,9},{9,1},{17,25},{25,17},{2,10},{10... | collective-permute-start | bytes 61448 | tf_op jit(solution)/shard_map/ppermute | solution.py:436
  0.0 5.1 %collective-permute-start.2 = (f32[10,512]{1,0:T(8,128)}, f32[10,512]{1,0:T(8,128)S(1)}, u32[]{:S(2)}, u32[]{:S(2)}) collective-permute-start(f32[10,512]{1,0:T(8,128)} %nodes_hbm.1), channel_id=1, source_target_pairs={{0,24},{8,16},{16,8},{24,0},{1,25},{9,17},{17,9},{25,1},{2,26},{10... | collective-permute-start | bytes 61448 | tf_op jit(solution)/shard_map/ppermute | solution.py:436
  2.4 3.3 %collective-permute-start.1 = (f32[10,512]{1,0:T(8,128)}, f32[10,512]{1,0:T(8,128)S(1)}, u32[]{:S(2)}, u32[]{:S(2)}) collective-permute-start(f32[10,512]{1,0:T(8,128)} %nodes_hbm.1), channel_id=1, source_target_pairs={{0,16},{8,24},{16,0},{24,8},{1,17},{9,25},{17,1},{25,9},{2,18},{10... | collective-permute-start | bytes 61448 | tf_op jit(solution)/shard_map/ppermute | solution.py:436
  5.8 6.5 %collective-permute-start.5 = (f32[4,40,128]{2,1,0:T(8,128)S(1)}, f32[4,40,128]{2,1,0:T(8,128)S(1)}, u32[]{:S(2)}, u32[]{:S(2)}) collective-permute-start(f32[4,40,128]{2,1,0:T(8,128)S(1)} %pad_maximum_fusion.1.mine_ref), channel_id=1, source_target_pairs={{0,6},{1,7},{2,4},{3,5},{4,2},{5,3},{6,0},{7,1},{8,14},{9,15},{10,... | collective-permute-start | bytes 245768 | tf_op jit(solution)/shard_map/ppermute | solution.py:436
  9.2 7.1 %collective-permute-start.4 = (f32[4,40,128]{2,1,0:T(8,128)S(1)}, f32[4,40,128]{2,1,0:T(8,128)S(1)}, u32[]{:S(2)}, u32[]{:S(2)}) collective-permute-start(f32[4,40,128]{2,1,0:T(8,128)S(1)} %pad_maximum_fusion.1.mine_ref), channel_id=1, source_target_pairs={{0,4},{1,5},{2,6},{3,7},{4,0},{5,1},{6,2},{7,3},{8,12},{9,13},{10,... | collective-permute-start | bytes 245768 | tf_op jit(solution)/shard_map/ppermute | solution.py:436
  9.2 7.1 %collective-permute-start.3 = (f32[4,40,128]{2,1,0:T(8,128)S(1)}, f32[4,40,128]{2,1,0:T(8,128)S(1)}, u32[]{:S(2)}, u32[]{:S(2)}) collective-permute-start(f32[4,40,128]{2,1,0:T(8,128)S(1)} %pad_maximum_fusion.1.mine_ref), channel_id=1, source_target_pairs={{0,2},{1,3},{2,0},{3,1},{4,6},{5,7},{6,4},{7,5},{8,10},{9,11},{10,... | collective-permute-start | bytes 245768 | tf_op jit(solution)/shard_map/ppermute | solution.py:436
  9.6 6.8 %collective-permute-start.6 = (f32[4,40,128]{2,1,0:T(8,128)S(1)}, f32[4,40,128]{2,1,0:T(8,128)S(1)}, u32[]{:S(2)}, u32[]{:S(2)}) collective-permute-start(f32[4,40,128]{2,1,0:T(8,128)S(1)} %pad_maximum_fusion.1.mine_ref), channel_id=1, source_target_pairs={{0,1},{1,0},{2,3},{3,2},{4,5},{5,4},{6,7},{7,6},{8,9},{9,8},{10,11... | collective-permute-start | bytes 245768 | tf_op jit(solution)/shard_map/ppermute | solution.py:436
  16.4 7.3 %copy-start = (s32[1,2048]{1,0:T(1,128)S(1)}, s32[1,2048]{1,0:T(1,128)}, u32[]{:S(2)}) copy-start(s32[1,2048]{1,0:T(1,128)} %slot_ref.1) | copy-start | bytes 24580
  22.1 1.6 %collective-permute-start.7 = (f32[12,40,128]{2,1,0:T(8,128)S(1)}, f32[12,40,128]{2,1,0:T(8,128)S(1)}, u32[]{:S(2)}, u32[]{:S(2)}) collective-permute-start(f32[12,40,128]{2,1,0:T(8,128)S(1)} %pad_maximum_fusion.mine_ref), channel_id=1, source_target_pairs={{0,1},{1,0},{2,3},{3,2},{4,5},{5,4},{6,7},{7,6},{8,9},{9,8},{10,11... | collective-permute-start | bytes 737288 | tf_op jit(solution)/shard_map/ppermute | solution.py:436
